TPU v7x, 128 devices: a whole 4x4x4 slice. The times are simulated.
128 devices in a mesh: dp: 16 (over x, z_lo, core), tensor: 8 (over y, z_hi).
Axes of the slice: x: 4, y: 4, z: 4 (z_hi: 2, z_lo: 2; z = z_hi * 2 + z_lo), core: 2. Of those that a mesh axis runs over, the one named last changes fastest.
Arguments:
- activations: bfloat16 [6144, 16384], P(('dp', 'tensor')), may hold values from -6 to 6
- out_grad: bfloat16 [6144, 16384], P('dp', 'tensor'), may hold values from -0.1875 to 0.1875
- block_ids: int32 [8, 12], replicated, may hold values from 0 to 127, as said below
- owner_map: int32 [16, 4], replicated, may hold values from 0 to 1, as said below
- master: float32 [1024, 16384], P('dp', 'tensor'), may hold values from -3 to 3
- moment: float32 [1024, 16384], P('dp', 'tensor'), may hold values from -3 to 3
- second: float32 [1024, 16384], P('dp', 'tensor'), may hold values from 0.01 to 2
Outputs:
- new_master: float32 [1024, 16384], P('dp', 'tensor')
- new_moment: float32 [1024, 16384], P('dp', 'tensor')
- new_second: float32 [1024, 16384], P('dp', 'tensor')
- hot_weights: bfloat16 [1024, 16384], P('dp')
- cold_recv: float32 [8192, 16384], P('dp', 'tensor')
Inputs may be any that keep to these rules, and one draw needn't show every extreme that they name: `block_ids`: the 12 block numbers in a row are distinct. `owner_map`: each row has between 1 and 3 ones; some row has exactly 3 ones and some row exactly 1.
All inputs are finite; a program needn't handle non-finite values.
Results may differ from a plain program's by a relative error of at most 0.006.
Values may be sent and summed in bfloat16 or wider, within the bound.
A program may use at most 128 MiB of HBM per device.

v0:
```python
import jax
import jax.numpy as jnp
from jax import lax
from jax.sharding import PartitionSpec as P

D = 16384
BLOCK = 128
HOT = 8
COLD = 4


BETA_ONE = 0.9
BETA_TWO = 0.95
ADAM_EPS = 1e-08
LEARN_RATE = 0.01
DECAY = 0.1
CORRECT_ONE = 1.0 - 0.9**10
CORRECT_TWO = 1.0 - 0.95**10


def in_blocks(shard, dim, devices):
    before, after = (shard.shape[:dim], shard.shape[dim + 1 :])
    return jnp.moveaxis(shard.reshape(*before, devices, -1, *after), dim, 0)


def summed_on_arrival(shard, axis, dim):
    pieces = in_blocks(shard, dim, lax.axis_size(axis))
    arrived = lax.all_to_all(pieces, axis, split_axis=0, concat_axis=0, tiled=True)
    return arrived.astype(jnp.float32).sum(axis=0)


def laid_out(pieces, dim):
    pieces = jnp.moveaxis(pieces, 0, dim)
    dims = pieces.shape
    return pieces.reshape(*dims[:dim], dims[dim] * dims[dim + 1], *dims[dim + 2 :])


def copy_for_each(shard, axis):
    devices = lax.axis_size(axis)
    return lax.all_to_all(
        jnp.broadcast_to(shard[None], (devices, *shard.shape)), axis, 0, 0, tiled=True
    )


def gathered_copies(shard, axis, dim):
    return laid_out(copy_for_each(shard, axis), dim)


def from_behind(block, axis, distance):
    devices = range(lax.axis_size(axis))
    route = [((i - distance) % len(devices), i) for i in devices]
    return lax.ppermute(block, axis, route)


def pick_blocks(tok_rows, block_row):
    shaped = tok_rows.reshape(tok_rows.shape[0], D // BLOCK, BLOCK)
    return shaped[:, block_row, :].reshape(tok_rows.shape[0], block_row.shape[0] * BLOCK)


def per_device(activations, out_grad, block_ids, owner_map, master, moment, second):
    qlocal = out_grad.shape[1]
    hot_count = HOT * BLOCK
    outgoing = jax.vmap(lambda block_row: pick_blocks(activations, block_row))(block_ids)
    received = lax.all_to_all(outgoing, "tensor", split_axis=0, concat_axis=0, tiled=True)
    chosen = received.reshape(received.shape[0] * received.shape[1], received.shape[2])
    hot_cols = chosen[:, :hot_count]
    cold_cols = chosen[:, hot_count:]
    contract = (((0,), (0,)), ((), ()))
    grad = summed_on_arrival(
        lax.dot_general(hot_cols, out_grad, contract, preferred_element_type=jnp.float32).astype(
            jnp.bfloat16
        ),
        "dp",
        0,
    )
    cold_part = lax.dot_general(cold_cols, out_grad, contract, preferred_element_type=jnp.float32)
    cold_part = cold_part.astype(jnp.bfloat16).reshape(COLD, BLOCK * qlocal)
    new_moment = BETA_ONE * moment + (1.0 - BETA_ONE) * grad
    new_second = BETA_TWO * second + (1.0 - BETA_TWO) * grad * grad
    update = new_moment / CORRECT_ONE / (jnp.sqrt(new_second / CORRECT_TWO) + ADAM_EPS)
    new_master = master - LEARN_RATE * (update + DECAY * master)
    hot_weights = gathered_copies(new_master.astype(jnp.bfloat16), "tensor", 1)
    dp_index = lax.axis_index("dp")
    dp_count = lax.axis_size("dp")
    prev_owner = lax.dynamic_index_in_dim(
        owner_map, (dp_index + dp_count - 1) % dp_count, 0, keepdims=False
    )
    next_owner = lax.dynamic_index_in_dim(owner_map, (dp_index + 1) % dp_count, 0, keepdims=False)
    from_prev = from_behind(cold_part, "dp", 1)
    from_next = from_behind(cold_part, "dp", -1)
    total = jnp.where((prev_owner == 1)[:, None], from_prev.astype(jnp.float32), 0.0)
    total = total + jnp.where((next_owner == 0)[:, None], from_next.astype(jnp.float32), 0.0)
    cold_recv = total.reshape(COLD * BLOCK, qlocal)
    return (new_master, new_moment, new_second, hot_weights, cold_recv)


def solution(mesh):
    return jax.shard_map(
        per_device,
        mesh=mesh,
        in_specs=(
            P(("dp", "tensor"), None),
            P("dp", "tensor"),
            P(),
            P(),
            P("dp", "tensor"),
            P("dp", "tensor"),
            P("dp", "tensor"),
        ),
        out_specs=(
            P("dp", "tensor"),
            P("dp", "tensor"),
            P("dp", "tensor"),
            P("dp", None),
            P("dp", "tensor"),
        ),
        check_vma=False,
    )
```

profile of v0, /device:TPU:1, one launch (start us, length us, event | category | flops | bytes accessed | tf_op | source)
XLA Modules:
  0.0 169.7 jit_solution(2237382083334977902)
XLA Ops:
  0.6 0.0 copy-start
  0.6 0.0 copy-start.5
  0.7 2.9 %copy_bitcast_fusion = bf16[48,128,128]{2,0,1:T(8,128)(2,1)} fusion(bf16[48,16384]{1,0:T(8,128)(2,1)} %param.7), kind=kLoop, calls=%fused_computation.5 | loop fusion | bytes 3145728 | tf_op jit(solution)/shard_map/vmap()/reshape | solution.py:56
  3.6 0.0 copy-done.5
  3.6 0.1 reshape.55
  3.7 2.2 %gather_fusion = bf16[96,48,128]{2,1,0:T(8,128)(2,1)S(1)} fusion(bf16[48,128,128]{2,0,1:T(8,128)(2,1)} %copy_bitcast_fusion, s32[1024]{0:T(1024)S(1)} %pad_clamp_fusion), kind=kCustom, calls=%fused_computation | custom fusion | bytes 2359680 | tf_op jit(solution)/shard_map/vmap()/gather | solution.py:57
  5.9 0.2 copy.25
  6.1 25.2 %all_to_all.15 = bf16[8,48,1536]{2,1,0:T(8,128)(2,1)S(1)} all-to-all(bf16[8,48,1536]{2,1,0:T(8,128)(2,1)S(1)} %bitcast.20), channel_id=1, replica_groups=mesh['dp'=16,'tensor'=8] {'tensor'}, dimensions={0} | all-to-all | bytes 2359296 | tf_op jit(solution)/shard_map/all_to_all | solution.py:64
  31.4 0.0 copy-done
  31.4 4.4 %convolution_convert_fusion = bf16[1024,2048]{1,0:T(8,128)(2,1)} fusion(bf16[384,2048]{1,0:T(8,128)(2,1)S(1)} %copy-done, bf16[384,1536]{1,0:T(8,128)(2,1)S(1)} %bitcast.23), kind=kOutput, calls=%fused_computation.3 | convolution fusion | flops 1612709888 | bytes 6553600 | tf_op jit(solution)/shard_map/dot_general | solution.py:70
  35.7 7.1 %all-to-all-start.1 = ((bf16[16,64,2048]{2,1,0:T(8,128)(2,1)}), bf16[16,64,2048]{2,1,0:T(8,128)(2,1)}, u32[]{:S(2)}, u32[]{:S(2)}) async-start(bf16[16,64,2048]{2,1,0:T(8,128)(2,1)} %bitcast.21), calls=%async_computation.1 | async-start | bytes 8388608 | tf_op jit(solution)/shard_map/all_to_all | solution.py:28
  42.8 2.6 %convolution_convert_fusion.1 = bf16[512,2048]{1,0:T(8,128)(2,1)} fusion(bf16[384,2048]{1,0:T(8,128)(2,1)S(1)} %copy-done, bf16[384,1536]{1,0:T(8,128)(2,1)S(1)} %bitcast.24), kind=kOutput, calls=%fused_computation.4 | convolution fusion | flops 806354944 | bytes 4063232 | tf_op jit(solution)/shard_map/dot_general | solution.py:76
  45.4 0.0 copy-start.4
  45.4 4.5 %reshape.51 = bf16[4,262144]{1,0:T(4,128)(2,1)} reshape(bf16[512,2048]{1,0:T(8,128)(2,1)} %convolution_convert_fusion.1) | data formatting | bytes 4194304 | tf_op jit(solution)/shard_map/reshape | solution.py:77
  50.0 0.2 collective-permute-start.1
  50.1 1.6 collective-permute-start
  51.7 0.0 copy-done.4
  51.7 0.2 fusion.3
  52.0 0.0 copy-start.1
  52.0 0.0 copy-start.2
  52.0 0.0 copy-start.3
  52.0 44.1 %all-to-all-done.1 = bf16[16,64,2048]{2,1,0:T(8,128)(2,1)} async-done(((bf16[16,64,2048]{2,1,0:T(8,128)(2,1)}), bf16[16,64,2048]{2,1,0:T(8,128)(2,1)}, u32[]{:S(2)}, u32[]{:S(2)}) %all-to-all-start.1) | async-done | bytes 4194336 | tf_op jit(solution)/shard_map/all_to_all | solution.py:28
  96.1 3.0 %convert_reduce_fusion = f32[64,2048]{1,0:T(8,128)S(1)} fusion(bf16[16,64,2048]{2,1,0:T(8,128)(2,1)} %all-to-all-done.1), kind=kLoop, calls=%fused_computation.1 | loop fusion | flops 4063232 | bytes 4718592 | tf_op jit(solution)/shard_map/reduce_sum | solution.py:29
  99.1 0.0 copy-done.1
  99.2 0.0 copy-done.2
  99.2 0.0 copy-done.3
  99.2 1.4 fusion.5
  100.6 1.6 broadcast_in_dim.30
  102.1 4.5 %all-to-all-start.2 = ((bf16[8,64,2048]{2,1,0:T(8,128)(2,1)}), bf16[8,64,2048]{2,1,0:T(8,128)(2,1)}, u32[]{:S(2)}, u32[]{:S(2)}) async-start(bf16[8,64,2048]{2,1,0:T(8,128)(2,1)} %broadcast_in_dim.30), calls=%async_computation.2 | async-start | bytes 4194304 | tf_op jit(solution)/shard_map/all_to_all | solution.py:40
  106.7 48.3 %collective-permute-done.1 = bf16[4,262144]{1,0:T(4,128)(2,1)} collective-permute-done((bf16[4,262144]{1,0:T(4,128)(2,1)}, bf16[4,262144]{1,0:T(4,128)(2,1)}, u32[]{:S(2)}, u32[]{:S(2)}) %collective-permute-start.1) | collective-permute-done | bytes 2097184 | tf_op jit(solution)/shard_map/ppermute | solution.py:52
  155.0 0.0 collective-permute-done
  155.0 4.5 %select_add_fusion = f32[4,262144]{1,0:T(4,128)} fusion(bf16[4,262144]{1,0:T(4,128)(2,1)} %collective-permute-done.1, bf16[4,262144]{1,0:T(4,128)(2,1)} %collective-permute-done, pred[4]{0:T(512)(128)(4,1)S(1)} %get-tuple-element.6, pred[4]{0:T(512)(128)(4,1)S(1)} %get-tuple-element.5), kind=kLoop, calls=%fused_computation.2 | loop fusion | flops 5242880 | bytes 8388616 | tf_op jit(solution)/shard_map/add | solution.py:92
  159.5 7.1 %reshape.52 = f32[512,2048]{1,0:T(8,128)} reshape(f32[4,262144]{1,0:T(4,128)} %select_add_fusion) | data formatting | bytes 8388608 | tf_op jit(solution)/shard_map/reshape | solution.py:93
  166.5 0.0 all-to-all-done.2
  166.5 3.2 %copy.22 = bf16[8,8,8,2048]{3,2,0,1:T(8,128)(2,1)} copy(bf16[8,8,8,2048]{3,2,1,0:T(8,128)(2,1)} %bitcast.10) | data formatting | bytes 4194304 | tf_op jit(solution)/shard_map/reshape | solution.py:35
  (2 shorter events, 0.0 us)
Async XLA Ops:
  0.6 30.7 %copy-start = (bf16[384,2048]{1,0:T(8,128)(2,1)S(1)}, bf16[384,2048]{1,0:T(8,128)(2,1)}, u32[]{:S(2)}) copy-start(bf16[384,2048]{1,0:T(8,128)(2,1)} %param.8) | copy-start | bytes 4718596
  0.6 3.0 %copy-start.5 = (s32[8,12]{1,0:T(8,128)S(1)}, s32[8,12]{1,0:T(8,128)}, u32[]{:S(2)}) copy-start(s32[8,12]{1,0:T(8,128)} %param.9) | copy-start | bytes 1156
  35.7 60.4 %all-to-all-start.1 = ((bf16[16,64,2048]{2,1,0:T(8,128)(2,1)}), bf16[16,64,2048]{2,1,0:T(8,128)(2,1)}, u32[]{:S(2)}, u32[]{:S(2)}) async-start(bf16[16,64,2048]{2,1,0:T(8,128)(2,1)} %bitcast.21), calls=%async_computation.1 | async-start | bytes 8388608 | tf_op jit(solution)/shard_map/all_to_all | solution.py:28
  45.4 6.3 %copy-start.4 = (s32[16,4]{0,1:T(4,128)S(1)}, s32[16,4]{0,1:T(4,128)}, u32[]{:S(2)}) copy-start(s32[16,4]{0,1:T(4,128)} %param.10) | copy-start | bytes 772
  50.0 105.0 %collective-permute-start.1 = (bf16[4,262144]{1,0:T(4,128)(2,1)}, bf16[4,262144]{1,0:T(4,128)(2,1)}, u32[]{:S(2)}, u32[]{:S(2)}) collective-permute-start(bf16[4,262144]{1,0:T(4,128)(2,1)} %reshape.51), channel_id=1, source_target_pairs={{8,0},{16,8},{24,16},{32,24},{40,32},{48,40},{56,48},{64,56},{72,6... | collective-permute-start | bytes 6291464 | tf_op jit(solution)/shard_map/ppermute | solution.py:52
  50.1 104.9 %collective-permute-start = (bf16[4,262144]{1,0:T(4,128)(2,1)}, bf16[4,262144]{1,0:T(4,128)(2,1)}, u32[]{:S(2)}, u32[]{:S(2)}) collective-permute-start(bf16[4,262144]{1,0:T(4,128)(2,1)} %reshape.51), channel_id=1, source_target_pairs={{120,0},{0,8},{8,16},{16,24},{24,32},{32,40},{40,48},{48,56},{56,6... | collective-permute-start | bytes 6291464 | tf_op jit(solution)/shard_map/ppermute | solution.py:52
  52.0 47.2 %copy-start.1 = (f32[64,2048]{1,0:T(8,128)S(1)}, f32[64,2048]{1,0:T(8,128)}, u32[]{:S(2)}) copy-start(f32[64,2048]{1,0:T(8,128)} %param.11) | copy-start | bytes 1572868
  52.0 47.2 %copy-start.2 = (f32[64,2048]{1,0:T(8,128)S(1)}, f32[64,2048]{1,0:T(8,128)}, u32[]{:S(2)}) copy-start(f32[64,2048]{1,0:T(8,128)} %param.12) | copy-start | bytes 1572868
  52.0 47.2 %copy-start.3 = (f32[64,2048]{1,0:T(8,128)S(1)}, f32[64,2048]{1,0:T(8,128)}, u32[]{:S(2)}) copy-start(f32[64,2048]{1,0:T(8,128)} %param.13) | copy-start | bytes 1572868
  102.1 64.4 %all-to-all-start.2 = ((bf16[8,64,2048]{2,1,0:T(8,128)(2,1)}), bf16[8,64,2048]{2,1,0:T(8,128)(2,1)}, u32[]{:S(2)}, u32[]{:S(2)}) async-start(bf16[8,64,2048]{2,1,0:T(8,128)(2,1)} %broadcast_in_dim.30), calls=%async_computation.2 | async-start | bytes 4194304 | tf_op jit(solution)/shard_map/all_to_all | solution.py:40
where the time goes:
time: 170 us
  waiting for transfers between devices  92.5 us (54%)
  blocking collectives  25.2 us (15%)
  local copies, waits for them, and re-layouts  21.8 us (13%)
  starting transfers between devices  13.4 us (8%)
  other arithmetic  9.08 us (5%)
  matrix products  6.99 us (4%)
    ppermute x2, waiting for transfers between devices, from_behind(): return lax.ppermute(block, axis, route)  48.3 us
    all_to_all x1, waiting for transfers between devices, summed_on_arrival(): lax.all_to_all(pieces, axis, split_axis=0, concat_axis=0, tiled=True)  44.1 us
    all_to_all x1, blocking collectives, per_device(): lax.all_to_all(outgoing, 'tensor', split_axis=0, concat_axis=0, tiled=True)  25.2 us
    all_to_all x1, starting transfers between devices, summed_on_arrival(): lax.all_to_all(pieces, axis, split_axis=0, concat_axis=0, tiled=True)  7.1 us
    reshape x1, local copies, waits for them, and re-layouts, per_device(): cold_recv = total.reshape(COLD * BLOCK, qlocal)  7.08 us
    reshape x1, local copies, waits for them, and re-layouts, per_device(): cold_part = cold_part.astype(jnp.bfloat16).reshape(COLD, BLOCK * qlocal)  4.54 us
    all_to_all x1, starting transfers between devices, copy_for_each(): lax.all_to_all(jnp.broadcast_to(shard[None], (devices, *shard.shape)), ax...  4.52 us
    add x1, other arithmetic, per_device(): total + jnp.where((next_owner == 0)[:, None], from_next.astype(jnp.float3...  4.45 us
  transfers between devices with their start and end apart: 4, of which 2 were waited for; matrix products, arithmetic and copies ran while one was open for 15% of the time, Pallas kernels for 0%

commit v1 on v0

v1 whole, which is shorter than its diff:
```python
import jax
import jax.numpy as jnp
from jax import lax
from jax.experimental import pallas as pl
from jax.experimental.pallas import tpu as pltpu
from jax.sharding import PartitionSpec as P

D = 16384
BLOCK = 128
HOT = 8
COLD = 4
SENT = 3
HALF = BLOCK // 2
CHUNKS = 4
EARLY = 2
MIDDLE = 3

BETA_ONE = 0.9
BETA_TWO = 0.95
ADAM_EPS = 1e-08
LEARN_RATE = 0.01
DECAY = 0.1
CORRECT_ONE = 1.0 - 0.9**10
CORRECT_TWO = 1.0 - 0.95**10

OFFSETS = ((2, 1), (1, 1), (3, 1), (0, 1), (2, 0), (1, 0), (3, 0))
CONTRACT = (((1,), (0,)), ((), ()))
F32 = jnp.float32
BF16 = jnp.bfloat16


def slots(own, index):
    ones = [own[index, k] for k in range(COLD)]
    seen, places = jnp.int32(0), []
    for k in range(COLD):
        places.append(seen)
        seen = seen + ones[k]
    places = [jnp.where(ones[k] == 1, places[k], seen + k - places[k]) for k in range(COLD)]
    return ones, places


def pick(ids, own, act, hot, cold):
    _, mine = slots(own, lax.axis_index("dp"))

    def columns(block):
        return act[:, pl.ds(pl.multiple_of(block * BLOCK, BLOCK), BLOCK)]

    def group_step(group, carry):
        for k in range(HOT):
            hot[group, :, k * BLOCK : (k + 1) * BLOCK] = columns(ids[group, k])
        for slot in range(COLD):
            block = jnp.int32(0)
            for k in range(COLD):
                block = block + jnp.where(mine[k] == slot, ids[group, HOT + k], 0)
            cold[group, :, slot * BLOCK : (slot + 1) * BLOCK] = columns(block)
        return carry

    lax.fori_loop(0, hot.shape[0], group_step, 0)


def kernel(
    send_hot, send_cold, og_h, ma_h, mo_h, se_h,
    oma_h, omo_h, ose_h, ohw_h, prev_h, next_h,
    og, state, hot_in, cold_in,
    prod, pair, quads, a_in, b_in, z_out, z_in, weights,
    part0, part1, part2, part3, load_sem, out_sem,
    hs_sem, hr_sem, cs_sem, cr_sem, ds_sem, dr_sem, as_sem, ar_sem, bs_sem, br_sem,
    zs_sem, zr_sem, ps_sem, pr_sem, ns_sem, nr_sem, gs_sem, gr_sem,
):
    rows, qlocal = send_hot.shape[1], og.shape[1]
    width = qlocal // CHUNKS
    i = lax.axis_index("dp")
    t = lax.axis_index("tensor")
    x, zl, c = lax.div(i, 4), lax.rem(lax.div(i, 2), 2), lax.rem(i, 2)
    y, zh = lax.div(t, 2), lax.rem(t, 2)

    def device(x_, zl_, c_):
        return ((x_ * 2 + zl_) * 2 + c_, t)

    def tensor(dy, dz):
        return lax.rem(y + dy, 4) * 2 + lax.rem(zh + dz, 2)

    right, left = device(lax.rem(x + 1, 4), zl, c), device(lax.rem(x + 3, 4), zl, c)
    mate, across = device(x, zl, 1 - c), device(x, 1 - zl, c)
    after, before = (lax.rem(i + 1, 16), t), (lax.rem(i + 15, 16), t)
    far = (lax.rem(i + 15 + 2 * c, 16), t)

    def remote(src, dst, send, recv, to):
        return pltpu.make_async_remote_copy(
            src_ref=src, dst_ref=dst, send_sem=send, recv_sem=recv, device_id=to,
            device_id_type=pl.DeviceIdType.MESH,
        )

    own_rows = pl.ds(pl.multiple_of(t * rows, rows), rows)
    loads = [
        pltpu.make_async_copy(send_hot.at[t], hot_in.at[own_rows], load_sem.at[0]),
        pltpu.make_async_copy(og_h, og, load_sem.at[1]),
        pltpu.make_async_copy(send_cold.at[t], cold_in.at[own_rows], load_sem.at[2]),
        pltpu.make_async_copy(ma_h, state.at[0], load_sem.at[3]),
        pltpu.make_async_copy(mo_h, state.at[1], load_sem.at[4]),
        pltpu.make_async_copy(se_h, state.at[2], load_sem.at[5]),
    ]
    for load in loads:
        load.start()

    barrier = pltpu.get_barrier_semaphore()
    peers = [(i, tensor(dy, dz)) for dy, dz in OFFSETS] + [right, left, mate, across, far]
    for peer in peers:
        pl.semaphore_signal(barrier, inc=1, device_id=peer, device_id_type=pl.DeviceIdType.MESH)

    pl.semaphore_wait(barrier, len(peers))

    def hot_copy(n):
        to = tensor(*OFFSETS[n])
        return remote(send_hot.at[to], hot_in.at[own_rows], hs_sem.at[n], hr_sem.at[n], (i, to))

    def cold_copy(n):
        to = tensor(*OFFSETS[n])
        return remote(send_cold.at[to], cold_in.at[own_rows], cs_sem.at[n], cr_sem.at[n], (i, to))

    for n in range(len(OFFSETS)):
        hot_copy(n).start()
    for n in range(len(OFFSETS)):
        cold_copy(n).start()
    loads[0].wait()
    loads[1].wait()
    for n in range(len(OFFSETS)):
        hot_copy(n).wait_recv()

    def mate_copy(k):
        return remote(prod.at[k, 1 - c], pair.at[k], ds_sem.at[k], dr_sem.at[k], mate)

    def hot_step(k, carry):
        dx = jnp.where(k < 2, 2, jnp.where(k < 4, 1, jnp.where(k < 6, 3, 0)))
        side = lax.rem(k, 2)
        side = jnp.where(k < 6, side, jnp.where(k == 6, 1 - zl, zl))
        block = lax.rem(x + dx, 4) * 2 + side
        picked = hot_in[:, pl.ds(pl.multiple_of(block * BLOCK, BLOCK), BLOCK)].T
        for n in range(CHUNKS):
            cols = pl.ds(n * width, width)
            got = lax.dot_general(picked, og[:, cols], CONTRACT, preferred_element_type=F32)
            got = got.astype(BF16)
            prod[k, 0, :, cols] = got[:HALF]
            prod[k, 1, :, cols] = got[HALF:]
        mate_copy(k).start()
        return carry

    lax.fori_loop(0, HOT, hot_step, 0)

    def pair_sum(k):
        mate_copy(k).wait_recv()
        return prod[k, c].astype(F32) + pair[k].astype(F32)

    a_right = remote(quads.at[0], a_in.at[0], as_sem.at[0], ar_sem.at[0], right)
    a_left = remote(quads.at[1], a_in.at[1], as_sem.at[1], ar_sem.at[1], left)
    b_right = [
        remote(quads.at[2 + k], b_in.at[k], bs_sem.at[k], br_sem.at[k], right) for k in range(2)
    ]
    b_left = [
        remote(quads.at[4 + k], b_in.at[2 + k], bs_sem.at[2 + k], br_sem.at[2 + k], left)
        for k in range(2)
    ]
    quads[0] = pair_sum(0).astype(BF16)
    a_right.start()
    quads[1] = pair_sum(1).astype(BF16)
    a_left.start()
    quads[3] = pair_sum(3).astype(BF16)
    b_right[1].start()
    quads[4] = pair_sum(4).astype(BF16)
    b_left[0].start()

    parts = (part0, part1, part2, part3)
    to_next = [
        remote(parts[n].at[0:SENT], prev_h.at[n], ps_sem.at[n], pr_sem.at[n], after)
        for n in range(CHUNKS)
    ]
    to_prev = [
        remote(parts[n].at[1 : 1 + SENT], next_h.at[n], ns_sem.at[n], nr_sem.at[n], before)
        for n in range(CHUNKS)
    ]

    def send_chunk(n):
        to_next[n].start()
        to_prev[n].start()

    loads[2].wait()
    for n in range(len(OFFSETS)):
        cold_copy(n).wait_recv()
    for n in range(CHUNKS):
        cols = pl.ds(n * width, width)
        for slot in range(COLD):
            picked = cold_in[:, slot * BLOCK : (slot + 1) * BLOCK].T
            got = lax.dot_general(picked, og[:, cols], CONTRACT, preferred_element_type=F32)
            parts[n][slot] = got.astype(BF16)
        if n < EARLY:
            send_chunk(n)

    first = pair_sum(2)
    a_right.wait_recv()
    quads[2] = (first + a_in[0].astype(F32)).astype(BF16)
    b_right[0].start()
    second = pair_sum(5)
    a_left.wait_recv()
    quads[5] = (second + a_in[1].astype(F32)).astype(BF16)
    b_left[1].start()
    for copy in b_right + b_left:
        copy.wait_recv()

    def arrived(k, side):
        return b_in[side].astype(F32) + b_in[2 + side].astype(F32)

    z_copy = remote(z_out, z_in, zs_sem, zr_sem, across)
    z_out[...] = (pair_sum(6) + arrived(6, 1 - zl)).astype(BF16)
    z_copy.start()
    for n in range(EARLY, MIDDLE):
        send_chunk(n)
    mate_copy(7).wait_recv()
    for load in loads[3:]:
        load.wait()
    z_copy.wait_recv()

    step_rows = 16

    def adam_step(k, carry):
        at = pl.ds(pl.multiple_of(k * step_rows, step_rows), step_rows)
        grad = prod[7, c, at].astype(F32) + pair[7, at].astype(F32) + z_in[at].astype(F32)
        grad = grad + b_in[zl, at].astype(F32) + b_in[2 + zl, at].astype(F32)
        master = state[0, at]
        moment = BETA_ONE * state[1, at] + (1.0 - BETA_ONE) * grad
        second = BETA_TWO * state[2, at] + (1.0 - BETA_TWO) * grad * grad
        update = moment / CORRECT_ONE / (jnp.sqrt(second / CORRECT_TWO) + ADAM_EPS)
        master = master - LEARN_RATE * (update + DECAY * master)
        state[0, at] = master
        state[1, at] = moment
        state[2, at] = second
        weights[t, at] = master.astype(BF16)
        return carry

    lax.fori_loop(0, HALF // step_rows, adam_step, 0)

    half = qlocal // 2

    def whole(slot):
        return weights.at[slot]

    def gather(n, slot, to, part=None):
        ref = weights.at[slot] if part is None else weights.at[slot, :, pl.ds(part * half, half)]
        return remote(ref, ref, gs_sem.at[n], gr_sem.at[n], (i, to))

    up, down, other = tensor(1, 0), tensor(3, 0), tensor(0, 1)
    g_up = gather(0, t, up)
    g_down = gather(1, t, down)
    g_other = gather(2, t, other)
    g_up.start()
    g_down.start()
    g_other.start()
    for n in range(MIDDLE, CHUNKS):
        send_chunk(n)

    outs = [
        pltpu.make_async_copy(state.at[0], oma_h, out_sem.at[0]),
        pltpu.make_async_copy(state.at[1], omo_h, out_sem.at[1]),
        pltpu.make_async_copy(state.at[2], ose_h, out_sem.at[2]),
    ]
    for out in outs:
        out.start()

    g_up.wait_recv()
    f_up = gather(3, tensor(3, 0), up, 0)
    f_up.start()
    g_down.wait_recv()
    f_down = gather(4, tensor(1, 0), down, 1)
    f_down.start()
    g_other.wait_recv()
    o_up = gather(5, other, up)
    o_down = gather(6, other, down)
    o_up.start()
    o_down.start()

    o_up.wait_recv()
    of_up = gather(7, tensor(3, 1), up, 0)
    of_up.start()
    o_down.wait_recv()
    of_down = gather(8, tensor(1, 1), down, 1)
    of_down.start()

    f_up.wait_recv()
    f_down.wait_recv()
    of_up.wait_recv()
    of_down.wait_recv()
    out = pltpu.make_async_copy(weights, ohw_h, out_sem.at[3])
    out.start()
    outs.append(out)
    for n in range(CHUNKS):
        to_next[n].wait_recv()
        to_prev[n].wait_recv()

    for n in range(len(OFFSETS)):
        hot_copy(n).wait_send()
        cold_copy(n).wait_send()
    for k in range(HOT):
        mate_copy(k).wait_send()
    sends = [a_right, a_left, *b_right, *b_left, z_copy, *to_next, *to_prev]
    sends += [g_up, g_down, g_other, f_up, f_down, o_up, o_down, of_up, of_down]
    for copy in sends:
        copy.wait_send()
    for out in outs:
        out.wait()


def finish(
    own, ma_h, mo_h, se_h, hw_h, prev_h, next_h, oma_h, omo_h, ose_h, ohw_h, ocold_h,
    state, weights, prev, late, stage, in_sem, cold_sem, out_sem, done_sem,
):
    i = lax.axis_index("dp")
    width = prev.shape[-1]
    qlocal = width * CHUNKS
    chunks = []
    for n in range(CHUNKS):
        chunks.append(
            (
                pltpu.make_async_copy(prev_h.at[n], prev.at[n], cold_sem.at[n, 0]),
                pltpu.make_async_copy(next_h.at[n], late.at[n], cold_sem.at[n, 1]),
            )
        )
        for copy in chunks[n]:
            copy.start()
    ins = [
        pltpu.make_async_copy(ref, state.at[k], in_sem.at[k])
        for k, ref in enumerate((ma_h, mo_h, se_h))
    ]
    ins.append(pltpu.make_async_copy(hw_h, weights, in_sem.at[3]))
    for copy in ins:
        copy.start()
    ones_prev, place_prev = slots(own, lax.rem(i + 15, 16))
    ones_next, place_next = slots(own, lax.rem(i + 1, 16))
    outs = []
    for n in range(CHUNKS):
        for copy in chunks[n]:
            copy.wait()
        for k in range(COLD):
            a = prev[n, jnp.minimum(place_prev[k], SENT - 1)].astype(F32)
            b = late[n, jnp.maximum(place_next[k] - 1, 0)].astype(F32)
            a = jnp.where(ones_prev[k] == 1, a, 0.0)
            b = jnp.where(ones_next[k] == 0, b, 0.0)
            stage[n, k * BLOCK : (k + 1) * BLOCK] = a + b
        outs.append(
            pltpu.make_async_copy(
                stage.at[n], ocold_h.at[:, pl.ds(n * width, width)], done_sem.at[n]
            )
        )
        outs[-1].start()
        if n == 0:
            for copy in ins:
                copy.wait()
            for k, ref in enumerate((oma_h, omo_h, ose_h)):
                outs.append(pltpu.make_async_copy(state.at[k], ref, out_sem.at[k]))
                outs[-1].start()
            for slot in range(8):
                outs.append(
                    pltpu.make_async_copy(
                        weights.at[slot],
                        ohw_h.at[:, pl.ds(slot * qlocal, qlocal)],
                        out_sem.at[3 + slot],
                    )
                )
                outs[-1].start()
    for out in outs:
        out.wait()


def per_device(activations, out_grad, block_ids, owner_map, master, moment, second):
    rows, tokens, qlocal = activations.shape[0], out_grad.shape[0], out_grad.shape[1]
    width = qlocal // CHUNKS
    partners = len(OFFSETS)
    dma = pltpu.SemaphoreType.DMA
    any_space = pl.BlockSpec(memory_space=pl.ANY)
    smem = pl.BlockSpec(memory_space=pltpu.SMEM)
    like = jax.ShapeDtypeStruct
    arrived = like((CHUNKS, SENT, BLOCK, width), BF16)
    states = (like(master.shape, F32),) * 3
    vmem = pl.BlockSpec(memory_space=pltpu.VMEM)
    chosen = pl.pallas_call(
        pick,
        name="pick",
        out_shape=(like((8, rows, HOT * BLOCK), BF16), like((8, rows, COLD * BLOCK), BF16)),
        in_specs=[smem, smem, vmem],
        out_specs=(vmem, vmem),
        compiler_params=pltpu.CompilerParams(vmem_limit_bytes=16 * 1024 * 1024),
    )(block_ids, owner_map, activations)
    gathered = pl.pallas_call(
        kernel,
        name="exchange",
        out_shape=(*states, like((8, HALF, qlocal), BF16), arrived, arrived),
        in_specs=[any_space] * 6,
        out_specs=(any_space,) * 6,
        scratch_shapes=[
            pltpu.VMEM((tokens, qlocal), BF16),
            pltpu.VMEM((3, HALF, qlocal), F32),
            pltpu.VMEM((tokens, HOT * BLOCK), BF16),
            pltpu.VMEM((tokens, COLD * BLOCK), BF16),
            pltpu.VMEM((HOT, 2, HALF, qlocal), BF16),
            pltpu.VMEM((HOT, HALF, qlocal), BF16),
            pltpu.VMEM((6, HALF, qlocal), BF16),
            pltpu.VMEM((2, HALF, qlocal), BF16),
            pltpu.VMEM((4, HALF, qlocal), BF16),
            pltpu.VMEM((HALF, qlocal), BF16),
            pltpu.VMEM((HALF, qlocal), BF16),
            pltpu.VMEM((8, HALF, qlocal), BF16),
            *[pltpu.VMEM((COLD, BLOCK, width), BF16)] * CHUNKS,
            dma((6,)),
            dma((4,)),
            *[dma((partners,))] * 4,
            *[dma((HOT,))] * 2,
            *[dma((2,))] * 2,
            *[dma((4,))] * 2,
            *[dma] * 2,
            *[dma((CHUNKS,))] * 4,
            *[dma((9,))] * 2,
        ],
        compiler_params=pltpu.CompilerParams(
            collective_id=0, has_side_effects=True, vmem_limit_bytes=40 * 1024 * 1024
        ),
    )(*chosen, out_grad, master, moment, second)
    return pl.pallas_call(
        finish,
        name="finish",
        out_shape=(
            *states,
            like((HALF, 8 * qlocal), BF16),
            like((COLD * BLOCK, qlocal), F32),
        ),
        in_specs=[smem] + [any_space] * 6,
        out_specs=(any_space,) * 5,
        scratch_shapes=[
            pltpu.VMEM((3, HALF, qlocal), F32),
            pltpu.VMEM((8, HALF, qlocal), BF16),
            pltpu.VMEM(arrived.shape, BF16),
            pltpu.VMEM(arrived.shape, BF16),
            pltpu.VMEM((CHUNKS, COLD * BLOCK, width), F32),
            dma((4,)),
            dma((CHUNKS, 2)),
            dma((11,)),
            dma((CHUNKS,)),
        ],
        compiler_params=pltpu.CompilerParams(vmem_limit_bytes=24 * 1024 * 1024),
    )(owner_map, *gathered)


def solution(mesh):
    return jax.shard_map(
        per_device,
        mesh=mesh,
        in_specs=(
            P(("dp", "tensor"), None),
            P("dp", "tensor"),
            P(),
            P(),
            P("dp", "tensor"),
            P("dp", "tensor"),
            P("dp", "tensor"),
        ),
        out_specs=(
            P("dp", "tensor"),
            P("dp", "tensor"),
            P("dp", "tensor"),
            P("dp", None),
            P("dp", "tensor"),
        ),
        check_vma=False,
    )
```

time: 170 us -> 102 us (0.60)
  Pallas kernels: 0 us -> 94.5 us
  waiting for transfers between devices: 92.5 us -> 0 us
  blocking collectives: 25.2 us -> 0 us
  local copies, waits for them, and re-layouts: 21.8 us -> 6.25 us
  starting transfers between devices: 13.4 us -> 0 us
  other arithmetic: 9.08 us -> 0 us
  matrix products: 6.99 us -> 0 us
    pallas_call x0 -> x3, Pallas kernels: none -> 94.5 us  [the longest x1 87.4 us: per_device(): pl.pallas_call(kernel, name='exchange', out_shape=(*states, like((8, HALF...]
    ppermute x2 -> x0, waiting for transfers between devices: 48.3 us -> none  [from_behind(): return lax.ppermute(block, axis, route)]
    all_to_all x2 -> x0, waiting for transfers between devices: 44.1 us -> none  [the longest x1 44.1 us: summed_on_arrival(): lax.all_to_all(pieces, axis, split_axis=0, concat_axis=0, tiled=True)]
    all_to_all x1 -> x0, blocking collectives: 25.2 us -> none  [per_device(): lax.all_to_all(outgoing, 'tensor', split_axis=0, concat_axis=0, tiled=True)]
    reshape x5 -> x0, local copies, waits for them, and re-layouts: 17.9 us -> none  [the longest x1 7.08 us: per_device(): cold_recv = total.reshape(COLD * BLOCK, qlocal)]
    all_to_all x2 -> x0, starting transfers between devices: 11.6 us -> none  [the longest x1 7.1 us: summed_on_arrival(): lax.all_to_all(pieces, axis, split_axis=0, concat_axis=0, tiled=True)]
    dot_general x2 -> x0, matrix products: 6.99 us -> none  [the longest x1 4.39 us: per_device(): lax.dot_general(hot_cols, out_grad, contract, preferred_element_type=jnp....]
    unnamed x12 -> x13, local copies, waits for them, and re-layouts: 0.04 us -> 6.25 us
  transfers between devices with their start and end apart: 4 -> 0, of which waited for: 2 -> 0; matrix products, arithmetic and copies ran while one was open for 15% -> 0% of each run, Pallas kernels for 0% -> 0%
where the time goes in v1:
time: 102 us; the launch traced here: 101 us
  Pallas kernels  94.5 us (93%)
  local copies, waits for them, and re-layouts  6.25 us (6%)
    pallas_call x1, Pallas kernels, per_device(): pl.pallas_call(kernel, name='exchange', out_shape=(*states, like((8, HALF...  87.4 us
    unnamed x13, local copies, waits for them, and re-layouts  6.25 us
    pallas_call x1, Pallas kernels, per_device(): pl.pallas_call(finish, name='finish', out_shape=(*states, like((HALF, 8 *...  5.99 us

profile of v1, /device:TPU:1, one launch (start us, length us, event | category | flops | bytes accessed | tf_op | source)
XLA Modules:
  0.0 101.4 jit_solution(4292212538347995278)
XLA Ops:
  0.6 0.8 copy.13.own
  1.4 0.0 copy-start
  1.4 1.4 %copy-done = bf16[48,16384]{1,0:T(8,128)(2,1)S(1)} copy-done((bf16[48,16384]{1,0:T(8,128)(2,1)S(1)}, bf16[48,16384]{1,0:T(8,128)(2,1)}, u32[]{:S(2)}) %copy-start) | copy-done | bytes 1572888
  2.8 0.0 copy-start.5
  2.8 0.7 copy-done.5
  3.5 0.0 copy-start.1
  3.5 1.1 %pick.1 = (bf16[8,48,1024]{2,1,0:T(8,128)(2,1)S(1)}, bf16[8,48,512]{2,1,0:T(8,128)(2,1)S(1)}) custom-call(s32[8,12]{1,0:T(8,128)S(1)} %copy-done.5, s32[16,4]{1,0:T(8,128)S(1)} %copy.13.own, bf16[48,16384]{1,0:T(8,128)(2,1)S(1)} %copy-done), custom_call_target="tpu_custom_call" | custom-call | tf_op jit(solution)/shard_map/pick/pallas_call | solution.py:383
  4.6 0.3 copy-done.1
  4.9 0.0 copy-start.2
  4.9 1.0 %copy-done.2 = f32[64,2048]{1,0:T(8,128)S(1)} copy-done((f32[64,2048]{1,0:T(8,128)S(1)}, f32[64,2048]{1,0:T(8,128)}, u32[]{:S(2)}) %copy-start.2) | copy-done | bytes 524312
  5.9 0.0 copy-start.3
  5.9 1.0 %copy-done.3 = f32[64,2048]{1,0:T(8,128)S(1)} copy-done((f32[64,2048]{1,0:T(8,128)S(1)}, f32[64,2048]{1,0:T(8,128)}, u32[]{:S(2)}) %copy-start.3) | copy-done | bytes 524312
  7.0 0.0 copy-start.4
  7.0 1.0 %copy-done.4 = f32[64,2048]{1,0:T(8,128)S(1)} copy-done((f32[64,2048]{1,0:T(8,128)S(1)}, f32[64,2048]{1,0:T(8,128)}, u32[]{:S(2)}) %copy-start.4) | copy-done | bytes 524312
  8.0 87.4 %exchange.1 = (f32[64,2048]{1,0:T(8,128)S(1)}, f32[64,2048]{1,0:T(8,128)S(1)}, f32[64,2048]{1,0:T(8,128)S(1)}, bf16[8,64,2048]{2,1,0:T(8,128)(2,1)S(1)}, bf16[4,...) custom-call(bf16[8,48,1024]{2,1,0:T(8,128)(2,1)S(1)} %get-tuple-element.13.send_hot, ...), custom_call_target="tpu_custom_call" | custom-call | tf_op jit(solution)/shard_map/exchange/pallas_call | solution.py:391
  95.4 6.0 %finish.1 = (f32[64,2048]{1,0:T(8,128)}, f32[64,2048]{1,0:T(8,128)}, f32[64,2048]{1,0:T(8,128)}, bf16[64,16384]{1,0:T(8,128)(2,1)}, f32[512,2048]{1,0:T(8,128)}) custom-call(s32[16,4]{1,0:T(8,128)S(1)} %copy.13.own, f32[64,2048]{1,0:T(8,128)S(1)} %get-tuple-element.15.ma_h, f32[64,2048]{1,0:T(8,128)S(1)} %get-tuple-element.16.mo_h, ...), custom_call_target="tpu_custom_call" | custom-call | tf_op jit(solution)/shard_map/finish/pallas_call | solution.py:425
Async XLA Ops:
  1.4 1.4 %copy-start = (bf16[48,16384]{1,0:T(8,128)(2,1)S(1)}, bf16[48,16384]{1,0:T(8,128)(2,1)}, u32[]{:S(2)}) copy-start(bf16[48,16384]{1,0:T(8,128)(2,1)} %act.1) | copy-start | bytes 4718596
  2.8 0.7 copy-start.5
  3.5 1.4 %copy-start.1 = (bf16[384,2048]{1,0:T(8,128)(2,1)S(1)}, bf16[384,2048]{1,0:T(8,128)(2,1)}, u32[]{:S(2)}) copy-start(bf16[384,2048]{1,0:T(8,128)(2,1)} %og_h.1) | copy-start | bytes 4718596
  4.9 1.0 %copy-start.2 = (f32[64,2048]{1,0:T(8,128)S(1)}, f32[64,2048]{1,0:T(8,128)}, u32[]{:S(2)}) copy-start(f32[64,2048]{1,0:T(8,128)} %ma_h.1) | copy-start | bytes 1572868
  5.9 1.0 %copy-start.3 = (f32[64,2048]{1,0:T(8,128)S(1)}, f32[64,2048]{1,0:T(8,128)}, u32[]{:S(2)}) copy-start(f32[64,2048]{1,0:T(8,128)} %mo_h.1) | copy-start | bytes 1572868
  7.0 1.0 %copy-start.4 = (f32[64,2048]{1,0:T(8,128)S(1)}, f32[64,2048]{1,0:T(8,128)}, u32[]{:S(2)}) copy-start(f32[64,2048]{1,0:T(8,128)} %se_h.1) | copy-start | bytes 1572868

commit v2 on v0

v2 whole, which is shorter than its diff:
```python
import jax
import jax.numpy as jnp
from jax import lax
from jax.experimental import pallas as pl
from jax.experimental.pallas import tpu as pltpu
from jax.sharding import PartitionSpec as P

D = 16384
BLOCK = 128
HOT = 8
COLD = 4
SENT = 3
OWNED = 64
PARTS = 4
CHUNKS = 8
DIRECT = (6, 7, 8)
DIAGONAL = (2, 3, 8)

BETA_ONE = 0.9
BETA_TWO = 0.95
ADAM_EPS = 1e-08
LEARN_RATE = 0.01
DECAY = 0.1
CORRECT_ONE = 1.0 - 0.9**10
CORRECT_TWO = 1.0 - 0.95**10

OFFSETS = ((2, 1), (1, 1), (3, 1), (0, 1), (2, 0), (1, 0), (3, 0))
CONTRACT = (((1,), (0,)), ((), ()))
F32 = jnp.float32
BF16 = jnp.bfloat16


def place(i):
    return lax.div(i, 4), lax.rem(lax.div(i, 2), 2), lax.rem(i, 2)


def hot_block(k, x, zl):
    step = (2, 2, 1, 1, 3, 3, 0, 0)[k]
    side = (0, 1, 0, 1, 0, 1, 1 - zl, zl)[k]
    return lax.rem(x + step, 4) * 2 + side


def slots(own, index):
    ones = [own[k, index] for k in range(COLD)]
    seen, places = jnp.int32(0), []
    for k in range(COLD):
        places.append(seen)
        seen = seen + ones[k]
    places = [jnp.where(ones[k] == 1, places[k], seen + k - places[k]) for k in range(COLD)]
    return ones, places


def pick(ids, own, act_h, hot, cold, act, sem):
    load = pltpu.make_async_copy(act_h, act, sem)
    load.start()
    i = lax.axis_index("dp")
    x, zl, _ = place(i)
    _, mine = slots(own, i)
    load.wait()

    def columns(block):
        return act[:, pl.ds(pl.multiple_of(block * BLOCK, BLOCK), BLOCK)]

    def group_step(group, carry):
        for k in range(HOT):
            at = k % 2 * BLOCK
            hot[k // 2, group, :, at : at + BLOCK] = columns(ids[group, hot_block(k, x, zl)])
        for slot in range(COLD):
            block = jnp.int32(0)
            for k in range(COLD):
                block = block + jnp.where(mine[k] == slot, ids[group, HOT + k], 0)
            cold[group, :, slot * BLOCK : (slot + 1) * BLOCK] = columns(block)
        return carry

    lax.fori_loop(0, cold.shape[0], group_step, 0)


def exchange(
    send_hot, send_cold, og_h, ma_h, mo_h, se_h,
    oma_h, omo_h, ose_h, ohw_h, recv_h,
    og, state, hot_in, cold_in, prod, pair, quads, a_in, b_in, z_out, z_in, weights, parts,
    load_sem, out_sem, hs_sem, hr_sem, cs_sem, cr_sem, ds_sem, dr_sem, as_sem, ar_sem,
    bs_sem, br_sem, zs_sem, zr_sem, ns_sem, nr_sem, fs_sem, fr_sem, gs_sem, gr_sem,
):
    rows, qlocal = send_hot.shape[2], og.shape[1]
    width, half, quarter = qlocal // CHUNKS, qlocal // 2, qlocal // 4
    i = lax.axis_index("dp")
    t = lax.axis_index("tensor")
    x, zl, c = place(i)
    y, zh = lax.div(t, 2), lax.rem(t, 2)

    def device(x_, zl_, c_):
        return ((x_ * 2 + zl_) * 2 + c_, t)

    def tensor(dy, dz):
        return lax.rem(y + dy, 4) * 2 + lax.rem(zh + dz, 2)

    right, left = device(lax.rem(x + 1, 4), zl, c), device(lax.rem(x + 3, 4), zl, c)
    mate, across = device(x, zl, 1 - c), device(x, 1 - zl, c)
    far = (lax.rem(i + 15 + 2 * c, 16), t)

    started = []

    def remote(src, dst, send, recv, to):
        copy = pltpu.make_async_remote_copy(
            src_ref=src, dst_ref=dst, send_sem=send, recv_sem=recv, device_id=to,
            device_id_type=pl.DeviceIdType.MESH,
        )
        started.append(copy)
        return copy

    own_rows = pl.ds(pl.multiple_of(t * rows, rows), rows)
    load_og = pltpu.make_async_copy(og_h, og, load_sem.at[0])
    load_own = [
        pltpu.make_async_copy(send_hot.at[p, t], hot_in.at[p, own_rows], load_sem.at[1 + p])
        for p in range(PARTS)
    ]
    load_cold = pltpu.make_async_copy(send_cold.at[t], cold_in.at[own_rows], load_sem.at[5])
    load_state = [
        pltpu.make_async_copy(ref, state.at[k], load_sem.at[6 + k])
        for k, ref in enumerate((ma_h, mo_h, se_h))
    ]
    for load in (load_og, *load_own, load_cold, *load_state):
        load.start()

    barrier = pltpu.get_barrier_semaphore()
    peers = [(i, tensor(dy, dz)) for dy, dz in OFFSETS] + [right, left, mate, across, far]
    for peer in peers:
        pl.semaphore_signal(barrier, inc=1, device_id=peer, device_id_type=pl.DeviceIdType.MESH)
    pl.semaphore_wait(barrier, len(peers))

    hot_copies, cold_copies = [[] for _ in range(PARTS)], []
    for p in (0, 1, 2, None, 3):
        for n, offset in enumerate(OFFSETS):
            to = tensor(*offset)
            if p is None:
                src, dst = send_cold.at[to], cold_in.at[own_rows]
                copy = remote(src, dst, cs_sem.at[n], cr_sem.at[n], (i, to))
                cold_copies.append(copy)
            else:
                src, dst = send_hot.at[p, to], hot_in.at[p, own_rows]
                copy = remote(src, dst, hs_sem.at[p, n], hr_sem.at[p, n], (i, to))
                hot_copies[p].append(copy)
            copy.start()

    mate_copies = [
        remote(prod.at[p, 1 - c], pair.at[p], ds_sem.at[p], dr_sem.at[p], mate)
        for p in range(PARTS)
    ]

    def multiply(p):
        load_own[p].wait()
        for copy in hot_copies[p]:
            copy.wait_recv()
        picked = hot_in[p].T
        for n in range(4):
            cols = pl.ds(n * quarter, quarter)
            got = lax.dot_general(picked, og[:, cols], CONTRACT, preferred_element_type=F32)
            got = got.astype(BF16)
            for k in range(2):
                for core in range(2):
                    at = k * BLOCK + core * OWNED
                    prod[p, core, k, :, cols] = got[at : at + OWNED]
        mate_copies[p].start()

    def pair_sum(k, cols):
        p, k = k // 2, k % 2
        return prod[p, c, k, :, cols].astype(F32) + pair[p, k, :, cols].astype(F32)

    every = pl.ds(0, qlocal)
    halves = [pl.ds(h * half, half) for h in range(2)]
    a_right = remote(quads.at[0], a_in.at[0], as_sem.at[0], ar_sem.at[0], right)
    a_left = remote(quads.at[1], a_in.at[1], as_sem.at[1], ar_sem.at[1], left)
    b_right = remote(quads.at[3], b_in.at[1], bs_sem.at[0], br_sem.at[0], right)
    b_left = remote(quads.at[4], b_in.at[2], bs_sem.at[1], br_sem.at[1], left)
    m_right = [
        remote(
            quads.at[2, :, cols], b_in.at[0, :, cols], bs_sem.at[2 + h], br_sem.at[2 + h], right
        )
        for h, cols in enumerate(halves)
    ]
    m_left = [
        remote(quads.at[5, :, cols], b_in.at[3, :, cols], bs_sem.at[4 + h], br_sem.at[4 + h], left)
        for h, cols in enumerate(halves)
    ]

    load_og.wait()
    multiply(0)
    multiply(1)
    mate_copies[0].wait_recv()
    quads[0] = pair_sum(0, every).astype(BF16)
    a_right.start()
    quads[1] = pair_sum(1, every).astype(BF16)
    a_left.start()
    multiply(2)
    mate_copies[1].wait_recv()
    quads[3] = pair_sum(3, every).astype(BF16)
    b_right.start()
    mate_copies[2].wait_recv()
    quads[4] = pair_sum(4, every).astype(BF16)
    b_left.start()

    near_copies = [
        remote(parts.at[n, pl.ds(c, SENT)], recv_h.at[c, n], ns_sem.at[n], nr_sem.at[n], mate)
        for n in range(CHUNKS)
    ]
    far_copies = [
        remote(
            parts.at[n, pl.ds(1 - c, SENT)], recv_h.at[1 - c, n], fs_sem.at[n], fr_sem.at[n], far
        )
        for n in range(CHUNKS)
    ]

    def send_far(direct, first, last):
        if first < last:

            @pl.when(zl != c if direct else zl == c)
            def _():
                for n in range(first, last):
                    far_copies[n].start()

    load_cold.wait()
    for copy in cold_copies:
        copy.wait_recv()
    picked = cold_in[...].T
    for n in range(CHUNKS):
        cols = pl.ds(n * width, width)
        got = lax.dot_general(picked, og[:, cols], CONTRACT, preferred_element_type=F32)
        parts[n] = got.astype(BF16).reshape(COLD, BLOCK, width)
        if n < DIRECT[0]:
            send_far(True, n, n + 1)
    multiply(3)

    a_right.wait_recv()
    for h, cols in enumerate(halves):
        quads[2, :, cols] = (pair_sum(2, cols) + a_in[0, :, cols].astype(F32)).astype(BF16)
        m_right[h].start()
        if h == 0:
            a_left.wait_recv()
        quads[5, :, cols] = (pair_sum(5, cols) + a_in[1, :, cols].astype(F32)).astype(BF16)
        m_left[h].start()
    send_far(False, 0, DIAGONAL[0])
    for n in range(CHUNKS):
        near_copies[n].start()

    z_copies = [
        remote(z_out.at[:, cols], z_in.at[:, cols], zs_sem.at[h], zr_sem.at[h], across)
        for h, cols in enumerate(halves)
    ]
    mate_copies[3].wait_recv()
    b_right.wait_recv()
    b_left.wait_recv()
    for h, cols in enumerate(halves):
        m_right[h].wait_recv()
        m_left[h].wait_recv()
        total = b_in[1 - zl, :, cols].astype(F32) + b_in[3 - zl, :, cols].astype(F32)
        z_out[:, cols] = (pair_sum(6, cols) + total).astype(BF16)
        z_copies[h].start()
    send_far(True, DIRECT[0], DIRECT[1])
    send_far(False, DIAGONAL[0], DIAGONAL[1])
    for load in load_state:
        load.wait()

    up, down, other = tensor(1, 0), tensor(3, 0), tensor(0, 1)

    def gather(n, slot, to, h, part=None):
        if part is None:
            at = weights.at[slot, :, halves[h]]
        else:
            at = weights.at[slot, :, pl.ds(h * half + part * quarter, quarter)]
        return remote(at, at, gs_sem.at[h, n], gr_sem.at[h, n], (i, to))

    step_rows = 16

    def adam(h):
        cols = halves[h]

        def adam_step(k, carry):
            at = pl.ds(pl.multiple_of(k * step_rows, step_rows), step_rows)
            grad = prod[3, c, 1, at, cols].astype(F32) + pair[3, 1, at, cols].astype(F32)
            grad = grad + b_in[zl, at, cols].astype(F32) + b_in[2 + zl, at, cols].astype(F32)
            grad = grad + z_in[at, cols].astype(F32)
            master = state[0, at, cols]
            moment = BETA_ONE * state[1, at, cols] + (1.0 - BETA_ONE) * grad
            second = BETA_TWO * state[2, at, cols] + (1.0 - BETA_TWO) * grad * grad
            update = moment / CORRECT_ONE / (jnp.sqrt(second / CORRECT_TWO) + ADAM_EPS)
            master = master - LEARN_RATE * (update + DECAY * master)
            state[0, at, cols] = master
            state[1, at, cols] = moment
            state[2, at, cols] = second
            weights[t, at, cols] = master.astype(BF16)
            return carry

        lax.fori_loop(0, OWNED // step_rows, adam_step, 0)

    g_up, g_down, g_other = [], [], []
    for h in range(2):
        z_copies[h].wait_recv()
        adam(h)
        g_up.append(gather(0, t, up, h))
        g_down.append(gather(1, t, down, h))
        g_other.append(gather(2, t, other, h))
        g_other[h].start()
        g_up[h].start()
        g_down[h].start()
    send_far(True, DIRECT[1], DIRECT[2])
    send_far(False, DIAGONAL[1], DIAGONAL[2])

    outs = [
        pltpu.make_async_copy(state.at[k], ref, out_sem.at[k])
        for k, ref in enumerate((oma_h, omo_h, ose_h))
    ]
    for out in outs:
        out.start()

    last = []
    for h in range(2):
        g_up[h].wait_recv()
        last.append(gather(3, down, up, h, 0))
        last[-1].start()
        g_down[h].wait_recv()
        last.append(gather(4, up, down, h, 1))
        last[-1].start()
    o_up, o_down = [], []
    for h in range(2):
        g_other[h].wait_recv()
        o_up.append(gather(5, other, up, h))
        o_up[h].start()
        o_down.append(gather(6, other, down, h))
        o_down[h].start()
    for h in range(2):
        o_up[h].wait_recv()
        last.append(gather(7, tensor(3, 1), up, h, 0))
        last[-1].start()
        o_down[h].wait_recv()
        last.append(gather(8, tensor(1, 1), down, h, 1))
        last[-1].start()
    for copy in last:
        copy.wait_recv()
    out = pltpu.make_async_copy(weights, ohw_h, out_sem.at[3])
    out.start()
    outs.append(out)
    for copy in near_copies + far_copies:
        copy.wait_recv()
    for copy in started:
        copy.wait_send()
    for out in outs:
        out.wait()


def finish(own, ma, mo, se, hw, recv, oma_h, omo_h, ose_h, ohw_h, ocold_h, stage, out_sem, cold_sem):
    i = lax.axis_index("dp")
    width = recv.shape[-1]
    qlocal = width * CHUNKS
    outs = []

    def put(src, dst, sem):
        outs.append(pltpu.make_async_copy(src, dst, sem))
        outs[-1].start()

    for k, (src, dst) in enumerate(((ma, oma_h), (mo, omo_h), (se, ose_h))):
        put(src, dst, out_sem.at[k])
    for slot in range(8):
        put(hw.at[slot], ohw_h.at[:, pl.ds(slot * qlocal, qlocal)], out_sem.at[3 + slot])
    ones_prev, place_prev = slots(own, lax.rem(i + 15, 16))
    ones_next, place_next = slots(own, lax.rem(i + 1, 16))
    for n in range(CHUNKS):
        for k in range(COLD):
            a = recv[0, n, jnp.minimum(place_prev[k], SENT - 1)].astype(F32)
            b = recv[1, n, jnp.maximum(place_next[k] - 1, 0)].astype(F32)
            a = jnp.where(ones_prev[k] == 1, a, 0.0)
            b = jnp.where(ones_next[k] == 0, b, 0.0)
            stage[n, k * BLOCK : (k + 1) * BLOCK] = a + b
        put(stage.at[n], ocold_h.at[:, pl.ds(n * width, width)], cold_sem.at[n])
    for out in outs:
        out.wait()


def per_device(activations, out_grad, block_ids, owner_map, master, moment, second):
    rows, tokens, qlocal = activations.shape[0], out_grad.shape[0], out_grad.shape[1]
    width = qlocal // CHUNKS
    partners = len(OFFSETS)
    dma, like = pltpu.SemaphoreType.DMA, jax.ShapeDtypeStruct
    anywhere = pl.BlockSpec(memory_space=pl.ANY)
    hbm = pl.BlockSpec(memory_space=pltpu.HBM)
    smem = pl.BlockSpec(memory_space=pltpu.SMEM)
    vmem = pl.BlockSpec(memory_space=pltpu.VMEM)
    owners = owner_map.T
    chosen = pl.pallas_call(
        pick,
        name="pick",
        out_shape=(like((PARTS, 8, rows, 2 * BLOCK), BF16), like((8, rows, COLD * BLOCK), BF16)),
        in_specs=[smem, smem, hbm],
        out_specs=(vmem, vmem),
        scratch_shapes=[pltpu.VMEM((rows, D), BF16), dma],
        compiler_params=pltpu.CompilerParams(vmem_limit_bytes=16 * 1024 * 1024),
    )(block_ids, owners, activations)
    states = (like(master.shape, F32),) * 3
    gathered = pl.pallas_call(
        exchange,
        name="exchange",
        out_shape=(
            *states,
            like((8, OWNED, qlocal), BF16),
            like((2, CHUNKS, SENT, BLOCK, width), BF16),
        ),
        in_specs=[anywhere] * 2 + [hbm] * 4,
        out_specs=(anywhere,) * 5,
        scratch_shapes=[
            pltpu.VMEM((tokens, qlocal), BF16),
            pltpu.VMEM((3, OWNED, qlocal), F32),
            pltpu.VMEM((PARTS, tokens, 2 * BLOCK), BF16),
            pltpu.VMEM((tokens, COLD * BLOCK), BF16),
            pltpu.VMEM((PARTS, 2, 2, OWNED, qlocal), BF16),
            pltpu.VMEM((PARTS, 2, OWNED, qlocal), BF16),
            pltpu.VMEM((6, OWNED, qlocal), BF16),
            pltpu.VMEM((2, OWNED, qlocal), BF16),
            pltpu.VMEM((4, OWNED, qlocal), BF16),
            pltpu.VMEM((OWNED, qlocal), BF16),
            pltpu.VMEM((OWNED, qlocal), BF16),
            pltpu.VMEM((8, OWNED, qlocal), BF16),
            pltpu.VMEM((CHUNKS, COLD, BLOCK, width), BF16),
            dma((9,)),
            dma((4,)),
            *[dma((PARTS, partners))] * 2,
            *[dma((partners,))] * 2,
            *[dma((PARTS,))] * 2,
            *[dma((2,))] * 2,
            *[dma((6,))] * 2,
            *[dma((2,))] * 2,
            *[dma((CHUNKS,))] * 4,
            *[dma((2, 9))] * 2,
        ],
        compiler_params=pltpu.CompilerParams(
            collective_id=0, has_side_effects=True, vmem_limit_bytes=40 * 1024 * 1024
        ),
    )(*chosen, out_grad, master, moment, second)
    return pl.pallas_call(
        finish,
        name="finish",
        out_shape=(
            *states,
            like((OWNED, 8 * qlocal), BF16),
            like((COLD * BLOCK, qlocal), F32),
        ),
        in_specs=[smem] + [vmem] * 5,
        out_specs=(anywhere,) * 5,
        scratch_shapes=[
            pltpu.VMEM((CHUNKS, COLD * BLOCK, width), F32),
            dma((11,)),
            dma((CHUNKS,)),
        ],
        compiler_params=pltpu.CompilerParams(vmem_limit_bytes=24 * 1024 * 1024),
    )(owners, *gathered)


def solution(mesh):
    return jax.shard_map(
        per_device,
        mesh=mesh,
        in_specs=(
            P(("dp", "tensor"), None),
            P("dp", "tensor"),
            P(),
            P(),
            P("dp", "tensor"),
            P("dp", "tensor"),
            P("dp", "tensor"),
        ),
        out_specs=(
            P("dp", "tensor"),
            P("dp", "tensor"),
            P("dp", "tensor"),
            P("dp", None),
            P("dp", "tensor"),
        ),
        check_vma=False,
    )
```

time: 170 us -> 98 us (0.58)
  the two profiles are of different devices: /device:TPU:1 before, /device:TPU:2 now
where the time goes in v2:
time: 98 us; the launch traced here: 97.7 us
  Pallas kernels  91 us (93%)
  local copies, waits for them, and re-layouts  6.05 us (6%)
    pallas_call x1, Pallas kernels, per_device(): pl.pallas_call(exchange, name='exchange', out_shape=(*states, like((8, OW...  85.8 us
    unnamed x16, local copies, waits for them, and re-layouts  6.05 us
    pallas_call x1, Pallas kernels, per_device(): pl.pallas_call(finish, name='finish', out_shape=(*states, like((OWNED, 8...  3.9 us

profile of v2, /device:TPU:2, one launch (start us, length us, event | category | flops | bytes accessed | tf_op | source)
XLA Modules:
  0.0 97.7 jit_solution(1121571085706338526)
XLA Ops:
  0.6 0.0 copy-start
  0.6 1.4 %copy-done = bf16[48,16384]{1,0:T(8,128)(2,1)S(1)} copy-done((bf16[48,16384]{1,0:T(8,128)(2,1)S(1)}, bf16[48,16384]{1,0:T(8,128)(2,1)}, u32[]{:S(2)}) %copy-start) | copy-done | bytes 1572888
  2.0 0.0 copy-start.5
  2.0 0.7 copy-done.5
  2.7 0.0 copy-start.7
  2.7 0.7 copy-done.7
  3.4 0.0 copy-start.1
  3.4 1.2 %pick.1 = (bf16[4,8,48,256]{3,2,1,0:T(8,128)(2,1)S(1)}, bf16[8,48,512]{2,1,0:T(8,128)(2,1)S(1)}) custom-call(s32[8,12]{1,0:T(8,128)S(1)} %copy-done.7, s32[4,16]{1,0:T(4,128)S(1)} %bitcast.1, bf16[48,16384]{1,0:T(8,128)(2,1)S(1)} %copy-done), custom_call_target="tpu_custom_call" | custom-call | tf_op jit(solution)/shard_map/pick/pallas_call | solution.py:389
  4.7 0.2 copy-done.1
  4.8 0.0 copy-start.2
  4.8 1.0 %copy-done.2 = f32[64,2048]{1,0:T(8,128)S(1)} copy-done((f32[64,2048]{1,0:T(8,128)S(1)}, f32[64,2048]{1,0:T(8,128)}, u32[]{:S(2)}) %copy-start.2) | copy-done | bytes 524312
  5.9 0.0 copy-start.3
  5.9 1.0 %copy-done.3 = f32[64,2048]{1,0:T(8,128)S(1)} copy-done((f32[64,2048]{1,0:T(8,128)S(1)}, f32[64,2048]{1,0:T(8,128)}, u32[]{:S(2)}) %copy-start.3) | copy-done | bytes 524312
  6.9 0.0 copy-start.4
  6.9 1.0 %copy-done.4 = f32[64,2048]{1,0:T(8,128)S(1)} copy-done((f32[64,2048]{1,0:T(8,128)S(1)}, f32[64,2048]{1,0:T(8,128)}, u32[]{:S(2)}) %copy-start.4) | copy-done | bytes 524312
  7.9 0.0 copy-start.6
  7.9 85.8 %exchange.1 = (f32[64,2048]{1,0:T(8,128)S(1)}, f32[64,2048]{1,0:T(8,128)S(1)}, f32[64,2048]{1,0:T(8,128)S(1)}, bf16[8,64,2048]{2,1,0:T(8,128)(2,1)S(1)}, bf16[2,8,3,128,256]{4,3,2,1,0:T(8,128)(2,1)S(1)}) custom-call(bf16[4,8,48,256]{3,2,1,0:T(8,128)(2,1)S(1)} %get-tuple-element.12.send_hot, bf16[8,48,512]{2,1,0:T(8,128)(2,1)S(1)} %get-tuple-element.13.send_cold, ...), custom_call_target="tpu_custom_call" | custom-call | tf_op jit(solution)/shard_map/exchange/pallas_call | solution.py:399
  93.8 0.0 copy-done.6
  93.8 3.9 %finish.1 = (f32[64,2048]{1,0:T(8,128)}, f32[64,2048]{1,0:T(8,128)}, f32[64,2048]{1,0:T(8,128)}, bf16[64,16384]{1,0:T(8,128)(2,1)}, f32[512,2048]{1,0:T(8,128)}) custom-call(s32[4,16]{1,0:T(4,128)S(1)} %bitcast.2, f32[64,2048]{1,0:T(8,128)S(1)} %get-tuple-element.14.ma, f32[64,2048]{1,0:T(8,128)S(1)} %get-tuple-element.15.mo, ...), custom_call_target="tpu_custom_call" | custom-call | tf_op jit(solution)/shard_map/finish/pallas_call | solution.py:438
Async XLA Ops:
  0.6 1.4 %copy-start = (bf16[48,16384]{1,0:T(8,128)(2,1)S(1)}, bf16[48,16384]{1,0:T(8,128)(2,1)}, u32[]{:S(2)}) copy-start(bf16[48,16384]{1,0:T(8,128)(2,1)} %act_h.1) | copy-start | bytes 4718596
  2.0 0.7 copy-start.5
  2.7 0.7 copy-start.7
  3.4 1.4 %copy-start.1 = (bf16[384,2048]{1,0:T(8,128)(2,1)S(1)}, bf16[384,2048]{1,0:T(8,128)(2,1)}, u32[]{:S(2)}) copy-start(bf16[384,2048]{1,0:T(8,128)(2,1)} %og_h.1) | copy-start | bytes 4718596
  4.8 1.0 %copy-start.2 = (f32[64,2048]{1,0:T(8,128)S(1)}, f32[64,2048]{1,0:T(8,128)}, u32[]{:S(2)}) copy-start(f32[64,2048]{1,0:T(8,128)} %ma_h.1) | copy-start | bytes 1572868
  5.9 1.0 %copy-start.3 = (f32[64,2048]{1,0:T(8,128)S(1)}, f32[64,2048]{1,0:T(8,128)}, u32[]{:S(2)}) copy-start(f32[64,2048]{1,0:T(8,128)} %mo_h.1) | copy-start | bytes 1572868
  6.9 1.0 %copy-start.4 = (f32[64,2048]{1,0:T(8,128)S(1)}, f32[64,2048]{1,0:T(8,128)}, u32[]{:S(2)}) copy-start(f32[64,2048]{1,0:T(8,128)} %se_h.1) | copy-start | bytes 1572868
  7.9 85.8 %copy-start.6 = (s32[16,4]{0,1:T(4,128)S(1)}, s32[16,4]{0,1:T(4,128)}, u32[]{:S(2)}) copy-start(s32[16,4]{0,1:T(4,128)} %param.10) | copy-start | bytes 772

commit v3 on v2

--- a/solution.py
+++ b/solution.py
@@ -13,8 +13,8 @@
 OWNED = 64
 PARTS = 4
 CHUNKS = 8
-DIRECT = (6, 7, 8)
-DIAGONAL = (2, 3, 8)
+DIRECT = (7, 7, 8, 8, 8, 8)
+RELAYED = (0, 0, 1, 4, 7, 8)
 
 BETA_ONE = 0.9
 BETA_TWO = 0.95
@@ -78,9 +78,10 @@
 def exchange(
     send_hot, send_cold, og_h, ma_h, mo_h, se_h,
     oma_h, omo_h, ose_h, ohw_h, recv_h,
-    og, state, hot_in, cold_in, prod, pair, quads, a_in, b_in, z_out, z_in, weights, parts,
+    og, state, hot_in, cold_in, prod, pair, quads, a_in, b_in, z_out, z_in, weights, parts, relay,
     load_sem, out_sem, hs_sem, hr_sem, cs_sem, cr_sem, ds_sem, dr_sem, as_sem, ar_sem,
-    bs_sem, br_sem, zs_sem, zr_sem, ns_sem, nr_sem, fs_sem, fr_sem, gs_sem, gr_sem,
+    bs_sem, br_sem, zs_sem, zr_sem, ns_sem, nr_sem, fs_sem, fr_sem, xs_sem, xr_sem,
+    gs_sem, gr_sem,
 ):
     rows, qlocal = send_hot.shape[2], og.shape[1]
     width, half, quarter = qlocal // CHUNKS, qlocal // 2, qlocal // 4
@@ -97,7 +98,7 @@
 
     right, left = device(lax.rem(x + 1, 4), zl, c), device(lax.rem(x + 3, 4), zl, c)
     mate, across = device(x, zl, 1 - c), device(x, 1 - zl, c)
-    far = (lax.rem(i + 15 + 2 * c, 16), t)
+    corner = device(x, 1 - zl, 1 - c)
 
     started = []
 
@@ -124,7 +125,7 @@
         load.start()
 
     barrier = pltpu.get_barrier_semaphore()
-    peers = [(i, tensor(dy, dz)) for dy, dz in OFFSETS] + [right, left, mate, across, far]
+    peers = [(i, tensor(dy, dz)) for dy, dz in OFFSETS] + [right, left, mate, across, corner]
     for peer in peers:
         pl.semaphore_signal(barrier, inc=1, device_id=peer, device_id_type=pl.DeviceIdType.MESH)
     pl.semaphore_wait(barrier, len(peers))
@@ -206,18 +207,38 @@
     ]
     far_copies = [
         remote(
-            parts.at[n, pl.ds(1 - c, SENT)], recv_h.at[1 - c, n], fs_sem.at[n], fr_sem.at[n], far
+            parts.at[n, pl.ds(1 - c, SENT)], recv_h.at[1 - c, n], fs_sem.at[n], fr_sem.at[n], corner
         )
         for n in range(CHUNKS)
     ]
-
-    def send_far(direct, first, last):
+    onward = device(lax.rem(x + 3 + 2 * c, 4), zl, c)
+    hop_copies = [
+        remote(parts.at[n, pl.ds(1 - c, SENT)], relay.at[n], xs_sem.at[n], xr_sem.at[n], onward)
+        for n in range(CHUNKS)
+    ]
+    relay_copies = [
+        remote(relay.at[n], recv_h.at[1 - c, n], fs_sem.at[n], fr_sem.at[n], corner)
+        for n in range(CHUNKS)
+    ]
+    del started[-2 * CHUNKS :]
+
+    def send_own(first, last):
         if first < last:
 
-            @pl.when(zl != c if direct else zl == c)
+            @pl.when(zl != c)
             def _():
                 for n in range(first, last):
                     far_copies[n].start()
+
+    def point(k):
+        send_own(DIRECT[k - 1], DIRECT[k])
+        if RELAYED[k - 1] < RELAYED[k]:
+
+            @pl.when(zl == c)
+            def _():
+                for n in range(RELAYED[k - 1], RELAYED[k]):
+                    hop_copies[n].wait_recv()
+                    relay_copies[n].start()
 
     load_cold.wait()
     for copy in cold_copies:
@@ -228,7 +249,7 @@
         got = lax.dot_general(picked, og[:, cols], CONTRACT, preferred_element_type=F32)
         parts[n] = got.astype(BF16).reshape(COLD, BLOCK, width)
         if n < DIRECT[0]:
-            send_far(True, n, n + 1)
+            send_own(n, n + 1)
     multiply(3)
 
     a_right.wait_recv()
@@ -239,7 +260,13 @@
             a_left.wait_recv()
         quads[5, :, cols] = (pair_sum(5, cols) + a_in[1, :, cols].astype(F32)).astype(BF16)
         m_left[h].start()
-    send_far(False, 0, DIAGONAL[0])
+
+    @pl.when(zl == c)
+    def _():
+        for n in range(CHUNKS):
+            hop_copies[n].start()
+
+    point(1)
     for n in range(CHUNKS):
         near_copies[n].start()
 
@@ -256,8 +283,7 @@
         total = b_in[1 - zl, :, cols].astype(F32) + b_in[3 - zl, :, cols].astype(F32)
         z_out[:, cols] = (pair_sum(6, cols) + total).astype(BF16)
         z_copies[h].start()
-    send_far(True, DIRECT[0], DIRECT[1])
-    send_far(False, DIAGONAL[0], DIAGONAL[1])
+    point(2)
     for load in load_state:
         load.wait()
 
@@ -303,8 +329,7 @@
         g_other[h].start()
         g_up[h].start()
         g_down[h].start()
-    send_far(True, DIRECT[1], DIRECT[2])
-    send_far(False, DIAGONAL[1], DIAGONAL[2])
+    point(3)
 
     outs = [
         pltpu.make_async_copy(state.at[k], ref, out_sem.at[k])
@@ -321,6 +346,7 @@
         g_down[h].wait_recv()
         last.append(gather(4, up, down, h, 1))
         last[-1].start()
+    point(4)
     o_up, o_down = [], []
     for h in range(2):
         g_other[h].wait_recv()
@@ -328,6 +354,7 @@
         o_up[h].start()
         o_down.append(gather(6, other, down, h))
         o_down[h].start()
+    point(5)
     for h in range(2):
         o_up[h].wait_recv()
         last.append(gather(7, tensor(3, 1), up, h, 0))
@@ -344,6 +371,12 @@
         copy.wait_recv()
     for copy in started:
         copy.wait_send()
+
+    @pl.when(zl == c)
+    def _():
+        for copy in hop_copies:
+            copy.wait_send()
+
     for out in outs:
         out.wait()
 
@@ -393,6 +426,7 @@
         in_specs=[smem, smem, hbm],
         out_specs=(vmem, vmem),
         scratch_shapes=[pltpu.VMEM((rows, D), BF16), dma],
+        cost_estimate=pl.CostEstimate(flops=2000000000, bytes_accessed=3000000, transcendentals=0),
         compiler_params=pltpu.CompilerParams(vmem_limit_bytes=16 * 1024 * 1024),
     )(block_ids, owners, activations)
     states = (like(master.shape, F32),) * 3
@@ -420,6 +454,7 @@
             pltpu.VMEM((OWNED, qlocal), BF16),
             pltpu.VMEM((8, OWNED, qlocal), BF16),
             pltpu.VMEM((CHUNKS, COLD, BLOCK, width), BF16),
+            pltpu.VMEM((CHUNKS, SENT, BLOCK, width), BF16),
             dma((9,)),
             dma((4,)),
             *[dma((PARTS, partners))] * 2,
@@ -428,7 +463,7 @@
             *[dma((2,))] * 2,
             *[dma((6,))] * 2,
             *[dma((2,))] * 2,
-            *[dma((CHUNKS,))] * 4,
+            *[dma((CHUNKS,))] * 6,
             *[dma((2, 9))] * 2,
         ],
         compiler_params=pltpu.CompilerParams(

time: 98 us -> 79.3 us (0.81)
  the two profiles are of different devices: /device:TPU:2 before, /device:TPU:0 now
where the time goes in v3:
time: 79.3 us; the launch traced here: 79.1 us
  Pallas kernels  75.1 us (95%)
  local copies, waits for them, and re-layouts  3.35 us (4%)
    pallas_call x1, Pallas kernels, per_device(): pl.pallas_call(exchange, name='exchange', out_shape=(*states, like((8, OW...  69.9 us
    pallas_call x1, Pallas kernels, per_device(): pl.pallas_call(finish, name='finish', out_shape=(*states, like((OWNED, 8...  3.9 us
    unnamed x16, local copies, waits for them, and re-layouts  3.35 us

profile of v3, /device:TPU:0, one launch (start us, length us, event | category | flops | bytes accessed | tf_op | source)
XLA Modules:
  0.0 79.1 jit_solution(7839922961149368623)
XLA Ops:
  0.6 0.0 copy-start.4
  0.6 0.7 copy-done.4
  1.3 0.0 copy-start.6
  1.3 1.4 %copy-done.6 = bf16[48,16384]{1,0:T(8,128)(2,1)S(1)} copy-done((bf16[48,16384]{1,0:T(8,128)(2,1)S(1)}, bf16[48,16384]{1,0:T(8,128)(2,1)}, u32[]{:S(2)}) %copy-start.6) | copy-done | bytes 1572888
  2.7 0.0 copy-start.7
  2.7 0.7 copy-done.7
  3.4 0.0 copy-start
  3.4 0.0 copy-start.1
  3.4 0.0 copy-start.2
  3.4 0.0 copy-start.3
  3.4 1.2 %pick.1 = (bf16[4,8,48,256]{3,2,1,0:T(8,128)(2,1)S(1)}, bf16[8,48,512]{2,1,0:T(8,128)(2,1)S(1)}) custom-call(s32[8,12]{1,0:T(8,128)S(1)} %copy-done.7, s32[4,16]{1,0:T(4,128)S(1)} %bitcast.1, bf16[48,16384]{1,0:T(8,128)(2,1)S(1)} %copy-done.6), custom_call_target="tpu_custom_call" | custom-call | flops 2000000000 | bytes 3000000 | tf_op jit(solution)/shard_map/pick/pallas_call | solution.py:422
  4.7 0.1 copy-done
  4.8 0.1 copy-done.1
  4.9 0.2 copy-done.2
  5.1 0.2 copy-done.3
  5.2 0.0 copy-start.5
  5.2 69.9 %exchange.1 = (f32[64,2048]{1,0:T(8,128)S(1)}, f32[64,2048]{1,0:T(8,128)S(1)}, f32[64,2048]{1,0:T(8,128)S(1)}, bf16[8,64,2048]{2,1,0:T(8,128)(2,1)S(1)}, bf16[2,8,3,128,256]{4,3,2,1,0:T(8,128)(2,1)S(1)}) custom-call(bf16[4,8,48,256]{3,2,1,0:T(8,128)(2,1)S(1)} %get-tuple-element.12.send_hot, bf16[8,48,512]{2,1,0:T(8,128)(2,1)S(1)} %get-tuple-element.13.send_cold, ...), custom_call_target="tpu_custom_call" | custom-call | tf_op jit(solution)/shard_map/exchange/pallas_call | solution.py:433
  75.2 0.0 copy-done.5
  75.2 3.9 %finish.1 = (f32[64,2048]{1,0:T(8,128)}, f32[64,2048]{1,0:T(8,128)}, f32[64,2048]{1,0:T(8,128)}, bf16[64,16384]{1,0:T(8,128)(2,1)}, f32[512,2048]{1,0:T(8,128)}) custom-call(s32[4,16]{1,0:T(4,128)S(1)} %bitcast.2, f32[64,2048]{1,0:T(8,128)S(1)} %get-tuple-element.14.ma, f32[64,2048]{1,0:T(8,128)S(1)} %get-tuple-element.15.mo, ...), custom_call_target="tpu_custom_call" | custom-call | tf_op jit(solution)/shard_map/finish/pallas_call | solution.py:473
Async XLA Ops:
  0.6 0.7 copy-start.4
  1.3 1.4 %copy-start.6 = (bf16[48,16384]{1,0:T(8,128)(2,1)S(1)}, bf16[48,16384]{1,0:T(8,128)(2,1)}, u32[]{:S(2)}) copy-start(bf16[48,16384]{1,0:T(8,128)(2,1)} %act_h.1) | copy-start | bytes 4718596
  2.7 0.7 copy-start.7
  3.4 1.4 %copy-start = (bf16[384,2048]{1,0:T(8,128)(2,1)S(1)}, bf16[384,2048]{1,0:T(8,128)(2,1)}, u32[]{:S(2)}) copy-start(bf16[384,2048]{1,0:T(8,128)(2,1)} %og_h.1) | copy-start | bytes 4718596
  3.4 1.5 %copy-start.1 = (f32[64,2048]{1,0:T(8,128)S(1)}, f32[64,2048]{1,0:T(8,128)}, u32[]{:S(2)}) copy-start(f32[64,2048]{1,0:T(8,128)} %ma_h.1) | copy-start | bytes 1572868
  3.4 1.7 %copy-start.2 = (f32[64,2048]{1,0:T(8,128)S(1)}, f32[64,2048]{1,0:T(8,128)}, u32[]{:S(2)}) copy-start(f32[64,2048]{1,0:T(8,128)} %mo_h.1) | copy-start | bytes 1572868
  3.4 1.8 %copy-start.3 = (f32[64,2048]{1,0:T(8,128)S(1)}, f32[64,2048]{1,0:T(8,128)}, u32[]{:S(2)}) copy-start(f32[64,2048]{1,0:T(8,128)} %se_h.1) | copy-start | bytes 1572868
  5.2 69.9 %copy-start.5 = (s32[16,4]{0,1:T(4,128)S(1)}, s32[16,4]{0,1:T(4,128)}, u32[]{:S(2)}) copy-start(s32[16,4]{0,1:T(4,128)} %param.10) | copy-start | bytes 772

commit v4 on v3

--- a/solution.py
+++ b/solution.py
@@ -12,9 +12,11 @@
 SENT = 3
 OWNED = 64
 PARTS = 4
+ORDER = (0, 1, None, 2, 3)
 CHUNKS = 8
-DIRECT = (7, 7, 8, 8, 8, 8)
-RELAYED = (0, 0, 1, 4, 7, 8)
+DIRECT = (0, 0, 2, 8, 8, 8, 8)
+DIAGONAL = (8, 8, 8, 8, 8, 8, 8)
+RELAYED = (0, 4, 6, 8, 8, 8, 8)
 
 BETA_ONE = 0.9
 BETA_TWO = 0.95
@@ -131,7 +133,7 @@
     pl.semaphore_wait(barrier, len(peers))
 
     hot_copies, cold_copies = [[] for _ in range(PARTS)], []
-    for p in (0, 1, 2, None, 3):
+    for p in ORDER:
         for n, offset in enumerate(OFFSETS):
             to = tensor(*offset)
             if p is None:
@@ -185,6 +187,61 @@
         for h, cols in enumerate(halves)
     ]
 
+    near_copies = [
+        remote(parts.at[n, pl.ds(c, SENT)], recv_h.at[c, n], ns_sem.at[n], nr_sem.at[n], mate)
+        for n in range(CHUNKS)
+    ]
+    far_copies = [
+        remote(
+            parts.at[n, pl.ds(1 - c, SENT)], recv_h.at[1 - c, n], fs_sem.at[n], fr_sem.at[n], corner
+        )
+        for n in range(CHUNKS)
+    ]
+    lift_copies = [
+        remote(parts.at[n, pl.ds(1 - c, SENT)], relay.at[n], fs_sem.at[n], fr_sem.at[n], corner)
+        for n in range(CHUNKS)
+    ]
+    onward = device(lax.rem(x + 1 + 2 * c, 4), zl, c)
+    relay_copies = [
+        remote(relay.at[n], recv_h.at[c, n], xs_sem.at[n], xr_sem.at[n], onward)
+        for n in range(CHUNKS)
+    ]
+    del started[-2 * CHUNKS :]
+
+    def send_far(direct, first, last):
+        if first < last:
+
+            @pl.when(zl != c if direct else zl == c)
+            def _():
+                for n in range(first, last):
+                    (far_copies if direct else lift_copies)[n].start()
+
+    def point(k):
+        if RELAYED[k - 1] < RELAYED[k]:
+
+            @pl.when(zl == c)
+            def _():
+                for n in range(RELAYED[k - 1], RELAYED[k]):
+                    lift_copies[n].wait_recv()
+                    relay_copies[n].start()
+
+        send_far(True, DIRECT[k - 1], DIRECT[k])
+        send_far(False, DIAGONAL[k - 1], DIAGONAL[k])
+
+    def cold_products():
+        load_cold.wait()
+        for copy in cold_copies:
+            copy.wait_recv()
+        picked = cold_in[...].T
+        for n in range(CHUNKS):
+            cols = pl.ds(n * width, width)
+            got = lax.dot_general(picked, og[:, cols], CONTRACT, preferred_element_type=F32)
+            parts[n] = got.astype(BF16).reshape(COLD, BLOCK, width)
+            if n < DIRECT[0]:
+                send_far(True, n, n + 1)
+            if n < DIAGONAL[0]:
+                send_far(False, n, n + 1)
+
     load_og.wait()
     multiply(0)
     multiply(1)
@@ -193,6 +250,7 @@
     a_right.start()
     quads[1] = pair_sum(1, every).astype(BF16)
     a_left.start()
+    cold_products()
     multiply(2)
     mate_copies[1].wait_recv()
     quads[3] = pair_sum(3, every).astype(BF16)
@@ -200,56 +258,6 @@
     mate_copies[2].wait_recv()
     quads[4] = pair_sum(4, every).astype(BF16)
     b_left.start()
-
-    near_copies = [
-        remote(parts.at[n, pl.ds(c, SENT)], recv_h.at[c, n], ns_sem.at[n], nr_sem.at[n], mate)
-        for n in range(CHUNKS)
-    ]
-    far_copies = [
-        remote(
-            parts.at[n, pl.ds(1 - c, SENT)], recv_h.at[1 - c, n], fs_sem.at[n], fr_sem.at[n], corner
-        )
-        for n in range(CHUNKS)
-    ]
-    onward = device(lax.rem(x + 3 + 2 * c, 4), zl, c)
-    hop_copies = [
-        remote(parts.at[n, pl.ds(1 - c, SENT)], relay.at[n], xs_sem.at[n], xr_sem.at[n], onward)
-        for n in range(CHUNKS)
-    ]
-    relay_copies = [
-        remote(relay.at[n], recv_h.at[1 - c, n], fs_sem.at[n], fr_sem.at[n], corner)
-        for n in range(CHUNKS)
-    ]
-    del started[-2 * CHUNKS :]
-
-    def send_own(first, last):
-        if first < last:
-
-            @pl.when(zl != c)
-            def _():
-                for n in range(first, last):
-                    far_copies[n].start()
-
-    def point(k):
-        send_own(DIRECT[k - 1], DIRECT[k])
-        if RELAYED[k - 1] < RELAYED[k]:
-
-            @pl.when(zl == c)
-            def _():
-                for n in range(RELAYED[k - 1], RELAYED[k]):
-                    hop_copies[n].wait_recv()
-                    relay_copies[n].start()
-
-    load_cold.wait()
-    for copy in cold_copies:
-        copy.wait_recv()
-    picked = cold_in[...].T
-    for n in range(CHUNKS):
-        cols = pl.ds(n * width, width)
-        got = lax.dot_general(picked, og[:, cols], CONTRACT, preferred_element_type=F32)
-        parts[n] = got.astype(BF16).reshape(COLD, BLOCK, width)
-        if n < DIRECT[0]:
-            send_own(n, n + 1)
     multiply(3)
 
     a_right.wait_recv()
@@ -260,12 +268,6 @@
             a_left.wait_recv()
         quads[5, :, cols] = (pair_sum(5, cols) + a_in[1, :, cols].astype(F32)).astype(BF16)
         m_left[h].start()
-
-    @pl.when(zl == c)
-    def _():
-        for n in range(CHUNKS):
-            hop_copies[n].start()
-
     point(1)
     for n in range(CHUNKS):
         near_copies[n].start()
@@ -367,16 +369,23 @@
     out = pltpu.make_async_copy(weights, ohw_h, out_sem.at[3])
     out.start()
     outs.append(out)
-    for copy in near_copies + far_copies:
+    point(6)
+    for copy in near_copies:
         copy.wait_recv()
+
+    @pl.when(zl != c)
+    def _():
+        for copy in far_copies:
+            copy.wait_recv()
+
+    @pl.when(zl == c)
+    def _():
+        for copy in relay_copies:
+            copy.wait_recv()
+            copy.wait_send()
+
     for copy in started:
         copy.wait_send()
-
-    @pl.when(zl == c)
-    def _():
-        for copy in hop_copies:
-            copy.wait_send()
-
     for out in outs:
         out.wait()
 

time: 79.3 us -> 78 us (0.984)
  the two profiles are of different devices: /device:TPU:0 before, /device:TPU:1 now
where the time goes in v4:
time: 78 us; the launch traced here: 77.8 us
  Pallas kernels  73.8 us (95%)
  local copies, waits for them, and re-layouts  3.35 us (4%)
    pallas_call x1, Pallas kernels, per_device(): pl.pallas_call(exchange, name='exchange', out_shape=(*states, like((8, OW...  68.6 us
    pallas_call x1, Pallas kernels, per_device(): pl.pallas_call(finish, name='finish', out_shape=(*states, like((OWNED, 8...  3.9 us
    unnamed x16, local copies, waits for them, and re-layouts  3.35 us

profile of v4, /device:TPU:1, one launch (start us, length us, event | category | flops | bytes accessed | tf_op | source)
XLA Modules:
  0.0 77.8 jit_solution(7053517958226269394)
XLA Ops:
  0.6 0.0 copy-start.4
  0.6 0.7 copy-done.4
  1.3 0.0 copy-start.6
  1.3 1.4 %copy-done.6 = bf16[48,16384]{1,0:T(8,128)(2,1)S(1)} copy-done((bf16[48,16384]{1,0:T(8,128)(2,1)S(1)}, bf16[48,16384]{1,0:T(8,128)(2,1)}, u32[]{:S(2)}) %copy-start.6) | copy-done | bytes 1572888
  2.7 0.0 copy-start.7
  2.7 0.7 copy-done.7
  3.4 0.0 copy-start
  3.4 0.0 copy-start.1
  3.4 0.0 copy-start.2
  3.4 0.0 copy-start.3
  3.4 1.2 %pick.1 = (bf16[4,8,48,256]{3,2,1,0:T(8,128)(2,1)S(1)}, bf16[8,48,512]{2,1,0:T(8,128)(2,1)S(1)}) custom-call(s32[8,12]{1,0:T(8,128)S(1)} %copy-done.7, s32[4,16]{1,0:T(4,128)S(1)} %bitcast.1, bf16[48,16384]{1,0:T(8,128)(2,1)S(1)} %copy-done.6), custom_call_target="tpu_custom_call" | custom-call | flops 2000000000 | bytes 3000000 | tf_op jit(solution)/shard_map/pick/pallas_call | solution.py:431
  4.7 0.1 copy-done
  4.8 0.1 copy-done.1
  4.9 0.2 copy-done.2
  5.1 0.2 copy-done.3
  5.2 0.0 copy-start.5
  5.2 68.6 %exchange.1 = (f32[64,2048]{1,0:T(8,128)S(1)}, f32[64,2048]{1,0:T(8,128)S(1)}, f32[64,2048]{1,0:T(8,128)S(1)}, bf16[8,64,2048]{2,1,0:T(8,128)(2,1)S(1)}, bf16[2,8,3,128,256]{4,3,2,1,0:T(8,128)(2,1)S(1)}) custom-call(bf16[4,8,48,256]{3,2,1,0:T(8,128)(2,1)S(1)} %get-tuple-element.12.send_hot, bf16[8,48,512]{2,1,0:T(8,128)(2,1)S(1)} %get-tuple-element.13.send_cold, ...), custom_call_target="tpu_custom_call" | custom-call | tf_op jit(solution)/shard_map/exchange/pallas_call | solution.py:442
  73.9 0.0 copy-done.5
  73.9 3.9 %finish.1 = (f32[64,2048]{1,0:T(8,128)}, f32[64,2048]{1,0:T(8,128)}, f32[64,2048]{1,0:T(8,128)}, bf16[64,16384]{1,0:T(8,128)(2,1)}, f32[512,2048]{1,0:T(8,128)}) custom-call(s32[4,16]{1,0:T(4,128)S(1)} %bitcast.2, f32[64,2048]{1,0:T(8,128)S(1)} %get-tuple-element.14.ma, f32[64,2048]{1,0:T(8,128)S(1)} %get-tuple-element.15.mo, ...), custom_call_target="tpu_custom_call" | custom-call | tf_op jit(solution)/shard_map/finish/pallas_call | solution.py:482
Async XLA Ops:
  0.6 0.7 copy-start.4
  1.3 1.4 %copy-start.6 = (bf16[48,16384]{1,0:T(8,128)(2,1)S(1)}, bf16[48,16384]{1,0:T(8,128)(2,1)}, u32[]{:S(2)}) copy-start(bf16[48,16384]{1,0:T(8,128)(2,1)} %act_h.1) | copy-start | bytes 4718596
  2.7 0.7 copy-start.7
  3.4 1.4 %copy-start = (bf16[384,2048]{1,0:T(8,128)(2,1)S(1)}, bf16[384,2048]{1,0:T(8,128)(2,1)}, u32[]{:S(2)}) copy-start(bf16[384,2048]{1,0:T(8,128)(2,1)} %og_h.1) | copy-start | bytes 4718596
  3.4 1.5 %copy-start.1 = (f32[64,2048]{1,0:T(8,128)S(1)}, f32[64,2048]{1,0:T(8,128)}, u32[]{:S(2)}) copy-start(f32[64,2048]{1,0:T(8,128)} %ma_h.1) | copy-start | bytes 1572868
  3.4 1.7 %copy-start.2 = (f32[64,2048]{1,0:T(8,128)S(1)}, f32[64,2048]{1,0:T(8,128)}, u32[]{:S(2)}) copy-start(f32[64,2048]{1,0:T(8,128)} %mo_h.1) | copy-start | bytes 1572868
  3.4 1.8 %copy-start.3 = (f32[64,2048]{1,0:T(8,128)S(1)}, f32[64,2048]{1,0:T(8,128)}, u32[]{:S(2)}) copy-start(f32[64,2048]{1,0:T(8,128)} %se_h.1) | copy-start | bytes 1572868
  5.2 68.6 %copy-start.5 = (s32[16,4]{0,1:T(4,128)S(1)}, s32[16,4]{0,1:T(4,128)}, u32[]{:S(2)}) copy-start(s32[16,4]{0,1:T(4,128)} %param.10) | copy-start | bytes 772

commit v5 on v4

--- a/solution.py
+++ b/solution.py
@@ -14,7 +14,7 @@
 PARTS = 4
 ORDER = (0, 1, None, 2, 3)
 CHUNKS = 8
-DIRECT = (0, 0, 2, 8, 8, 8, 8)
+DIRECT = (0, 0, 2, 4, 8, 8, 8)
 DIAGONAL = (8, 8, 8, 8, 8, 8, 8)
 RELAYED = (0, 4, 6, 8, 8, 8, 8)
 
@@ -436,7 +436,7 @@
         out_specs=(vmem, vmem),
         scratch_shapes=[pltpu.VMEM((rows, D), BF16), dma],
         cost_estimate=pl.CostEstimate(flops=2000000000, bytes_accessed=3000000, transcendentals=0),
-        compiler_params=pltpu.CompilerParams(vmem_limit_bytes=16 * 1024 * 1024),
+        compiler_params=pltpu.CompilerParams(vmem_limit_bytes=52 * 1024 * 1024),
     )(block_ids, owners, activations)
     states = (like(master.shape, F32),) * 3
     gathered = pl.pallas_call(

time: 78 us -> 77.7 us (level)
  local copies, waits for them, and re-layouts: 3.35 us -> 1.38 us
  Pallas kernels: 73.8 us -> 75.4 us
    unnamed x16 -> x12, local copies, waits for them, and re-layouts: 3.35 us -> 1.38 us
    pallas_call x1, Pallas kernels: 1.24 us -> 2.81 us  [per_device(): pl.pallas_call(pick, name='pick', out_shape=(like((PARTS, 8, rows, 2 * BL...]
where the time goes in v5:
time: 77.7 us; the launch traced here: 77.5 us
  Pallas kernels  75.4 us (97%)
  local copies, waits for them, and re-layouts  1.38 us (2%)
    pallas_call x1, Pallas kernels, per_device(): pl.pallas_call(exchange, name='exchange', out_shape=(*states, like((8, OW...  68.7 us
    pallas_call x1, Pallas kernels, per_device(): pl.pallas_call(finish, name='finish', out_shape=(*states, like((OWNED, 8...  3.9 us
    pallas_call x1, Pallas kernels, per_device(): pl.pallas_call(pick, name='pick', out_shape=(like((PARTS, 8, rows, 2 * BL...  2.81 us

profile of v5, /device:TPU:1, one launch (start us, length us, event | category | flops | bytes accessed | tf_op | source)
XLA Modules:
  0.0 77.5 jit_solution(9890639376619946521)
XLA Ops:
  0.6 0.0 copy-start.4
  0.6 0.7 copy-done.4
  1.3 0.0 copy-start.5
  1.3 0.7 copy-done.5
  2.0 0.0 copy-start
  2.0 0.0 copy-start.1
  2.0 0.0 copy-start.2
  2.0 0.0 copy-start.3
  2.0 2.8 %pick.1 = (bf16[4,8,48,256]{3,2,1,0:T(8,128)(2,1)S(1)}, bf16[8,48,512]{2,1,0:T(8,128)(2,1)S(1)}) custom-call(s32[8,12]{1,0:T(8,128)S(1)} %copy-done.5, s32[4,16]{1,0:T(4,128)S(1)} %bitcast.1, bf16[48,16384]{1,0:T(8,128)(2,1)} %act_h.1), custom_call_target="tpu_custom_call" | custom-call | flops 2000000000 | bytes 3000000 | tf_op jit(solution)/shard_map/pick/pallas_call | solution.py:431
  4.8 0.0 copy-done
  4.8 0.0 copy-done.1
  4.9 0.0 copy-done.2
  4.9 0.0 copy-done.3
  4.9 68.7 %exchange.1 = (f32[64,2048]{1,0:T(8,128)S(1)}, f32[64,2048]{1,0:T(8,128)S(1)}, f32[64,2048]{1,0:T(8,128)S(1)}, bf16[8,64,2048]{2,1,0:T(8,128)(2,1)S(1)}, bf16[2,8,3,128,256]{4,3,2,1,0:T(8,128)(2,1)S(1)}) custom-call(bf16[4,8,48,256]{3,2,1,0:T(8,128)(2,1)S(1)} %get-tuple-element.12.send_hot, bf16[8,48,512]{2,1,0:T(8,128)(2,1)S(1)} %get-tuple-element.13.send_cold, ...), custom_call_target="tpu_custom_call" | custom-call | tf_op jit(solution)/shard_map/exchange/pallas_call | solution.py:442
  73.6 3.9 %finish.1 = (f32[64,2048]{1,0:T(8,128)}, f32[64,2048]{1,0:T(8,128)}, f32[64,2048]{1,0:T(8,128)}, bf16[64,16384]{1,0:T(8,128)(2,1)}, f32[512,2048]{1,0:T(8,128)}) custom-call(s32[4,16]{1,0:T(4,128)S(1)} %bitcast.2, f32[64,2048]{1,0:T(8,128)S(1)} %get-tuple-element.14.ma, f32[64,2048]{1,0:T(8,128)S(1)} %get-tuple-element.15.mo, ...), custom_call_target="tpu_custom_call" | custom-call | tf_op jit(solution)/shard_map/finish/pallas_call | solution.py:482
Async XLA Ops:
  0.6 0.7 copy-start.4
  1.3 0.7 copy-start.5
  2.0 2.8 %copy-start = (bf16[384,2048]{1,0:T(8,128)(2,1)S(1)}, bf16[384,2048]{1,0:T(8,128)(2,1)}, u32[]{:S(2)}) copy-start(bf16[384,2048]{1,0:T(8,128)(2,1)} %og_h.1) | copy-start | bytes 4718596
  2.0 2.8 %copy-start.1 = (f32[64,2048]{1,0:T(8,128)S(1)}, f32[64,2048]{1,0:T(8,128)}, u32[]{:S(2)}) copy-start(f32[64,2048]{1,0:T(8,128)} %ma_h.1) | copy-start | bytes 1572868
  2.0 2.8 %copy-start.2 = (f32[64,2048]{1,0:T(8,128)S(1)}, f32[64,2048]{1,0:T(8,128)}, u32[]{:S(2)}) copy-start(f32[64,2048]{1,0:T(8,128)} %mo_h.1) | copy-start | bytes 1572868
  2.0 2.9 %copy-start.3 = (f32[64,2048]{1,0:T(8,128)S(1)}, f32[64,2048]{1,0:T(8,128)}, u32[]{:S(2)}) copy-start(f32[64,2048]{1,0:T(8,128)} %se_h.1) | copy-start | bytes 1572868

commit v6 on v5

--- a/solution.py
+++ b/solution.py
@@ -12,9 +12,9 @@
 SENT = 3
 OWNED = 64
 PARTS = 4
-ORDER = (0, 1, None, 2, 3)
+ORDER = (0, None, 1, 2, 3)
 CHUNKS = 8
-DIRECT = (0, 0, 2, 4, 8, 8, 8)
+DIRECT = (0, 0, 2, 8, 8, 8, 8)
 DIAGONAL = (8, 8, 8, 8, 8, 8, 8)
 RELAYED = (0, 4, 6, 8, 8, 8, 8)
 
@@ -244,13 +244,13 @@
 
     load_og.wait()
     multiply(0)
+    cold_products()
     multiply(1)
     mate_copies[0].wait_recv()
     quads[0] = pair_sum(0, every).astype(BF16)
     a_right.start()
     quads[1] = pair_sum(1, every).astype(BF16)
     a_left.start()
-    cold_products()
     multiply(2)
     mate_copies[1].wait_recv()
     quads[3] = pair_sum(3, every).astype(BF16)

time: 77.7 us -> 77.8 us (level)
  no operation moved by 1% of the time
where the time goes in v6:
time: 77.8 us; the launch traced here: 77.6 us
  Pallas kernels  75.6 us (97%)
  local copies, waits for them, and re-layouts  1.38 us (2%)
    pallas_call x1, Pallas kernels, per_device(): pl.pallas_call(exchange, name='exchange', out_shape=(*states, like((8, OW...  68.9 us
    pallas_call x1, Pallas kernels, per_device(): pl.pallas_call(finish, name='finish', out_shape=(*states, like((OWNED, 8...  3.9 us
    pallas_call x1, Pallas kernels, per_device(): pl.pallas_call(pick, name='pick', out_shape=(like((PARTS, 8, rows, 2 * BL...  2.81 us

profile of v6, /device:TPU:1, one launch (start us, length us, event | category | flops | bytes accessed | tf_op | source)
XLA Modules:
  0.0 77.6 jit_solution(9106241318517627074)
XLA Ops:
  0.6 0.0 copy-start.4
  0.6 0.7 copy-done.4
  1.3 0.0 copy-start.5
  1.3 0.7 copy-done.5
  2.0 0.0 copy-start
  2.0 0.0 copy-start.1
  2.0 0.0 copy-start.2
  2.0 0.0 copy-start.3
  2.0 2.8 %pick.1 = (bf16[4,8,48,256]{3,2,1,0:T(8,128)(2,1)S(1)}, bf16[8,48,512]{2,1,0:T(8,128)(2,1)S(1)}) custom-call(s32[8,12]{1,0:T(8,128)S(1)} %copy-done.5, s32[4,16]{1,0:T(4,128)S(1)} %bitcast.1, bf16[48,16384]{1,0:T(8,128)(2,1)} %act_h.1), custom_call_target="tpu_custom_call" | custom-call | flops 2000000000 | bytes 3000000 | tf_op jit(solution)/shard_map/pick/pallas_call | solution.py:431
  4.8 0.0 copy-done
  4.8 0.0 copy-done.1
  4.9 0.0 copy-done.2
  4.9 0.0 copy-done.3
  4.9 68.9 %exchange.1 = (f32[64,2048]{1,0:T(8,128)S(1)}, f32[64,2048]{1,0:T(8,128)S(1)}, f32[64,2048]{1,0:T(8,128)S(1)}, bf16[8,64,2048]{2,1,0:T(8,128)(2,1)S(1)}, bf16[2,8,3,128,256]{4,3,2,1,0:T(8,128)(2,1)S(1)}) custom-call(bf16[4,8,48,256]{3,2,1,0:T(8,128)(2,1)S(1)} %get-tuple-element.12.send_hot, bf16[8,48,512]{2,1,0:T(8,128)(2,1)S(1)} %get-tuple-element.13.send_cold, ...), custom_call_target="tpu_custom_call" | custom-call | tf_op jit(solution)/shard_map/exchange/pallas_call | solution.py:442
  73.7 3.9 %finish.1 = (f32[64,2048]{1,0:T(8,128)}, f32[64,2048]{1,0:T(8,128)}, f32[64,2048]{1,0:T(8,128)}, bf16[64,16384]{1,0:T(8,128)(2,1)}, f32[512,2048]{1,0:T(8,128)}) custom-call(s32[4,16]{1,0:T(4,128)S(1)} %bitcast.2, f32[64,2048]{1,0:T(8,128)S(1)} %get-tuple-element.14.ma, f32[64,2048]{1,0:T(8,128)S(1)} %get-tuple-element.15.mo, ...), custom_call_target="tpu_custom_call" | custom-call | tf_op jit(solution)/shard_map/finish/pallas_call | solution.py:482
Async XLA Ops:
  0.6 0.7 copy-start.4
  1.3 0.7 copy-start.5
  2.0 2.8 %copy-start = (bf16[384,2048]{1,0:T(8,128)(2,1)S(1)}, bf16[384,2048]{1,0:T(8,128)(2,1)}, u32[]{:S(2)}) copy-start(bf16[384,2048]{1,0:T(8,128)(2,1)} %og_h.1) | copy-start | bytes 4718596
  2.0 2.8 %copy-start.1 = (f32[64,2048]{1,0:T(8,128)S(1)}, f32[64,2048]{1,0:T(8,128)}, u32[]{:S(2)}) copy-start(f32[64,2048]{1,0:T(8,128)} %ma_h.1) | copy-start | bytes 1572868
  2.0 2.8 %copy-start.2 = (f32[64,2048]{1,0:T(8,128)S(1)}, f32[64,2048]{1,0:T(8,128)}, u32[]{:S(2)}) copy-start(f32[64,2048]{1,0:T(8,128)} %mo_h.1) | copy-start | bytes 1572868
  2.0 2.9 %copy-start.3 = (f32[64,2048]{1,0:T(8,128)S(1)}, f32[64,2048]{1,0:T(8,128)}, u32[]{:S(2)}) copy-start(f32[64,2048]{1,0:T(8,128)} %se_h.1) | copy-start | bytes 1572868

commit v7 on v6

--- a/solution.py
+++ b/solution.py
@@ -16,7 +16,7 @@
 CHUNKS = 8
 DIRECT = (0, 0, 2, 8, 8, 8, 8)
 DIAGONAL = (8, 8, 8, 8, 8, 8, 8)
-RELAYED = (0, 4, 6, 8, 8, 8, 8)
+RELAYED = (0, 2, 4, 6, 8, 8, 8)
 
 BETA_ONE = 0.9
 BETA_TWO = 0.95

time: 77.8 us -> 77.8 us (level)
  no operation moved by 1% of the time
where the time goes in v7:
time: 77.8 us; the launch traced here: 77.6 us
  Pallas kernels  75.6 us (97%)
  local copies, waits for them, and re-layouts  1.38 us (2%)
    pallas_call x1, Pallas kernels, per_device(): pl.pallas_call(exchange, name='exchange', out_shape=(*states, like((8, OW...  68.9 us
    pallas_call x1, Pallas kernels, per_device(): pl.pallas_call(finish, name='finish', out_shape=(*states, like((OWNED, 8...  3.9 us
    pallas_call x1, Pallas kernels, per_device(): pl.pallas_call(pick, name='pick', out_shape=(like((PARTS, 8, rows, 2 * BL...  2.81 us

profile of v7, /device:TPU:1, one launch (start us, length us, event | category | flops | bytes accessed | tf_op | source)
XLA Modules:
  0.0 77.6 jit_solution(17543064049039318812)
XLA Ops:
  0.6 0.0 copy-start.4
  0.6 0.7 copy-done.4
  1.3 0.0 copy-start.5
  1.3 0.7 copy-done.5
  2.0 0.0 copy-start
  2.0 0.0 copy-start.1
  2.0 0.0 copy-start.2
  2.0 0.0 copy-start.3
  2.0 2.8 %pick.1 = (bf16[4,8,48,256]{3,2,1,0:T(8,128)(2,1)S(1)}, bf16[8,48,512]{2,1,0:T(8,128)(2,1)S(1)}) custom-call(s32[8,12]{1,0:T(8,128)S(1)} %copy-done.5, s32[4,16]{1,0:T(4,128)S(1)} %bitcast.1, bf16[48,16384]{1,0:T(8,128)(2,1)} %act_h.1), custom_call_target="tpu_custom_call" | custom-call | flops 2000000000 | bytes 3000000 | tf_op jit(solution)/shard_map/pick/pallas_call | solution.py:431
  4.8 0.0 copy-done
  4.8 0.0 copy-done.1
  4.9 0.0 copy-done.2
  4.9 0.0 copy-done.3
  4.9 68.9 %exchange.1 = (f32[64,2048]{1,0:T(8,128)S(1)}, f32[64,2048]{1,0:T(8,128)S(1)}, f32[64,2048]{1,0:T(8,128)S(1)}, bf16[8,64,2048]{2,1,0:T(8,128)(2,1)S(1)}, bf16[2,8,3,128,256]{4,3,2,1,0:T(8,128)(2,1)S(1)}) custom-call(bf16[4,8,48,256]{3,2,1,0:T(8,128)(2,1)S(1)} %get-tuple-element.12.send_hot, bf16[8,48,512]{2,1,0:T(8,128)(2,1)S(1)} %get-tuple-element.13.send_cold, ...), custom_call_target="tpu_custom_call" | custom-call | tf_op jit(solution)/shard_map/exchange/pallas_call | solution.py:442
  73.7 3.9 %finish.1 = (f32[64,2048]{1,0:T(8,128)}, f32[64,2048]{1,0:T(8,128)}, f32[64,2048]{1,0:T(8,128)}, bf16[64,16384]{1,0:T(8,128)(2,1)}, f32[512,2048]{1,0:T(8,128)}) custom-call(s32[4,16]{1,0:T(4,128)S(1)} %bitcast.2, f32[64,2048]{1,0:T(8,128)S(1)} %get-tuple-element.14.ma, f32[64,2048]{1,0:T(8,128)S(1)} %get-tuple-element.15.mo, ...), custom_call_target="tpu_custom_call" | custom-call | tf_op jit(solution)/shard_map/finish/pallas_call | solution.py:482
Async XLA Ops:
  0.6 0.7 copy-start.4
  1.3 0.7 copy-start.5
  2.0 2.8 %copy-start = (bf16[384,2048]{1,0:T(8,128)(2,1)S(1)}, bf16[384,2048]{1,0:T(8,128)(2,1)}, u32[]{:S(2)}) copy-start(bf16[384,2048]{1,0:T(8,128)(2,1)} %og_h.1) | copy-start | bytes 4718596
  2.0 2.8 %copy-start.1 = (f32[64,2048]{1,0:T(8,128)S(1)}, f32[64,2048]{1,0:T(8,128)}, u32[]{:S(2)}) copy-start(f32[64,2048]{1,0:T(8,128)} %ma_h.1) | copy-start | bytes 1572868
  2.0 2.8 %copy-start.2 = (f32[64,2048]{1,0:T(8,128)S(1)}, f32[64,2048]{1,0:T(8,128)}, u32[]{:S(2)}) copy-start(f32[64,2048]{1,0:T(8,128)} %mo_h.1) | copy-start | bytes 1572868
  2.0 2.9 %copy-start.3 = (f32[64,2048]{1,0:T(8,128)S(1)}, f32[64,2048]{1,0:T(8,128)}, u32[]{:S(2)}) copy-start(f32[64,2048]{1,0:T(8,128)} %se_h.1) | copy-start | bytes 1572868
